TPU v7x, 128 devices: a whole 4x4x4 slice. The times are simulated.
128 devices in a mesh: dp: 16 (over z, x_lo, core), tensor: 8 (over x_hi, y).
Axes of the slice: x: 4 (x_hi: 2, x_lo: 2; x = x_hi * 2 + x_lo), y: 4, z: 4, core: 2. Of those that a mesh axis runs over, the one named last changes fastest.
Arguments:
- prompt_ids: int32 [16384], P(('dp', 'tensor')), may hold values from 0 to 128255
- prompt_lengths: int32 [32], replicated, may hold values from 1 to 512, as said below
- embed_table: bfloat16 [4096, 128256], P(('dp', 'tensor')), may hold values from -4 to 4
- norm_gain: float32 [4096], replicated, may hold values from 0.5 to 1.5
- w_query: bfloat16 [4096, 4096], P('dp', 'tensor'), may hold values from -3 to 3
- w_key: bfloat16 [4096, 1024], P('dp', 'tensor'), may hold values from -1 to 1
- w_value: bfloat16 [4096, 1024], P('dp', 'tensor'), may hold values from -0.09375 to 0.09375
- w_out: bfloat16 [4096, 4096], P('tensor', 'dp'), may hold values from -0.09375 to 0.09375
Outputs:
- hidden: bfloat16 [16384, 4096], P(('dp', 'tensor'))
- kv_cache: bfloat16 [128, 2, 512, 256], P(('dp', 'tensor'))
Inputs may be any that keep to these rules, and one draw needn't show every extreme that they name: `prompt_lengths`: each group's prompt has 1 to 512 live tokens, and some group's has 512.
All inputs are finite; a program needn't handle non-finite values.
Results may differ from a plain program's by a relative error of at most 0.0095.
Values may be sent and summed in bfloat16 or wider, within the bound.
A program may use at most 192 MiB of HBM per device.

v0:
```python
import jax
import jax.numpy as jnp
from jax import lax
from jax.sharding import Mesh
from jax.sharding import PartitionSpec as P

HEADS = 32
KVH = 8
HD = 128
TPG = 4
TENSOR = ("tensor_0", "tensor_1")
DP_TENSOR = ("dp_0", "dp_1", "dp_2", "tensor_0", "tensor_1")
DP = ("dp_0", "dp_1", "dp_2")


norm_eps = 1e-05
rope_theta = 500000.0


def piece_ends(length, count):
    turn = length // count
    if turn >= 8:
        turn -= turn % 8
    return [turn * k for k in range(1, count)]


def stacked_from(shard, axes, sequence):
    pieces = shard[None]
    for k in sequence:
        pieces = lax.all_gather(pieces, axes[k], axis=0, tiled=True)
    block = [lax.axis_size(axes[k]) for k in reversed(sequence)]
    pieces = pieces.reshape(*block, *shard.shape)
    turned = sorted(range(len(sequence)), key=lambda place: sequence[len(sequence) - 1 - place])
    return pieces.transpose(*turned, *range(len(sequence), pieces.ndim)).reshape(-1, *shard.shape)


def laid_out(pieces, dim):
    shape = list(pieces.shape[1:])
    shape[dim] *= pieces.shape[0]
    return jnp.moveaxis(pieces, 0, dim).reshape(shape)


def gather_at_once(shard, axes, dim):
    split_at = max(range(max(1, shard.ndim - 1)), key=lambda d: shard.shape[d])
    count, outs = (len(axes), [])
    for first, slab in enumerate(
        jnp.split(shard, piece_ends(shard.shape[split_at], count), axis=split_at)
    ):
        if slab.size:
            sequence = [(first - k) % count for k in range(count)]
            outs.append(stacked_from(slab, axes, sequence))
    return laid_out(jnp.concatenate(outs, axis=split_at + 1), dim)


def swapped(block, axis, apart):
    count = lax.axis_size(axis)
    route = []
    for low in range(count):
        high = low | 1 << apart
        if high != low and high < count:
            route += [(low, high), (high, low)]
    return lax.ppermute(block, axis, route)


def rotate(heads_in, positions):
    half = heads_in.shape[-1] // 2
    freq = rope_theta ** (-2.0 * jnp.arange(half, dtype=jnp.float32) / heads_in.shape[-1])
    angle = positions.astype(jnp.float32)[:, None] * freq[None, :]
    cosine = jnp.cos(angle)[:, None, :]
    sine = jnp.sin(angle)[:, None, :]
    first = heads_in[..., :half]
    second = heads_in[..., half:]
    return jnp.concatenate(
        [first * cosine - second * sine, second * cosine + first * sine], axis=-1
    )


def attend(query_rot, key_rot, value_rows, length):
    row_count = query_rot.shape[0]
    block = min(512, row_count)
    positions = jnp.arange(row_count, dtype=jnp.int32)

    def one_block(offset):
        scores = jnp.einsum(
            "qhgd,khd->hgqk", query_rot, key_rot, preferred_element_type=jnp.float32
        ) / jnp.sqrt(jnp.float32(HD))
        query_pos = offset + jnp.arange(block, dtype=jnp.int32)
        allowed = (positions[None, :] <= query_pos[:, None]) & (positions[None, :] < length)
        scores = jnp.where(allowed, scores, -1e30)
        biggest = jnp.max(scores, axis=-1, keepdims=True)
        expd = jnp.exp(scores - biggest)
        weights = (expd / jnp.sum(expd, axis=-1, keepdims=True)).astype(jnp.bfloat16)
        result = jnp.einsum(
            "hgqk,khd->qhgd", weights, value_rows, preferred_element_type=jnp.float32
        )
        return result.astype(jnp.bfloat16)

    starts = jnp.arange(0, row_count, block, dtype=jnp.int32)
    outs = lax.map(one_block, starts)
    return outs.reshape(row_count, -1)


def ordered_pair(mine, theirs, bit_index):
    upper_half = lax.axis_index(TENSOR) >> bit_index & 1 == 1
    first_half = jnp.where(upper_half, theirs, mine)
    second_half = jnp.where(upper_half, mine, theirs)
    return jnp.concatenate([first_half, second_half], axis=0)


def collect_blocks(shard, swapper):
    stacked = shard[None]
    stacked = ordered_pair(stacked, swapper(stacked, 2), 2)
    return stacked


def rms_normed(tokens_in, norm_gain):
    wide_in = tokens_in.astype(jnp.float32)
    scale = lax.rsqrt(jnp.mean(wide_in * wide_in, axis=1, keepdims=True) + norm_eps)
    return (wide_in * scale * norm_gain[None, :]).astype(jnp.bfloat16)


def lookup_rows(embed_table, token_ids):
    columns = embed_table.shape[0]
    vocab_size = embed_table.shape[1]
    packing = max(1, 128 // columns)
    token_major = embed_table.T.reshape(vocab_size // packing, packing * columns)
    fetched = jnp.take(token_major, token_ids // packing, axis=0).reshape(
        token_ids.shape[0], packing, columns
    )
    slot_ids = jnp.arange(packing, dtype=jnp.int32)
    wanted = (token_ids % packing)[:, None] == slot_ids[None, :]
    chosen = jnp.where(wanted[:, :, None], fetched, jnp.zeros_like(fetched))
    return jnp.sum(chosen, axis=1, dtype=jnp.bfloat16)


def shards(prompt_ids, prompt_lengths, embed_table, norm_gain, w_query, w_key, w_value, w_out):
    quarter = prompt_ids.shape[0]
    row_count = quarter * TPG
    devices = lax.axis_size(DP_TENSOR)
    columns = embed_table.shape[0]
    model_width = columns * devices
    member = lax.axis_index(TENSOR) % TPG
    group_index = (
        lax.axis_index(DP) * (lax.axis_size(TENSOR) // TPG) + lax.axis_index(TENSOR) // TPG
    )
    length = lax.dynamic_slice_in_dim(prompt_lengths, group_index, 1, 0)[0]
    all_ids = gather_at_once(prompt_ids, DP_TENSOR, 0)
    picked = lookup_rows(embed_table, all_ids)
    group_count = devices // TPG
    outgoing = jnp.broadcast_to(
        picked.reshape(group_count, 1, row_count, columns), (group_count, TPG, row_count, columns)
    )
    arrived = lax.all_to_all(
        outgoing.reshape(devices, row_count, columns),
        DP_TENSOR,
        split_axis=0,
        concat_axis=2,
        tiled=True,
    )
    group_rows = arrived.reshape(row_count, model_width)
    normed = rms_normed(group_rows, norm_gain)
    own_rows = lax.dynamic_slice_in_dim(group_rows, member * quarter, quarter, 0)
    query_width = w_query.shape[1]
    key_width = w_key.shape[1]
    packed = jnp.concatenate([w_query, w_key, w_value], axis=1)
    stacked = collect_blocks(packed, lambda values, bit_index: swapped(values, TENSOR, bit_index))
    projected = jnp.einsum(
        "rd,kdc->rkc",
        normed,
        lax.all_gather(stacked, DP, axis=1, tiled=True),
        preferred_element_type=jnp.float32,
    )
    blocks = projected.shape[1]
    local_heads = blocks * query_width // HD
    local_kv = blocks * key_width // HD
    positions = jnp.arange(row_count, dtype=jnp.int32)
    query = projected[:, :, :query_width].reshape(row_count, local_heads, HD)
    key_raw = projected[:, :, query_width : query_width + key_width]
    value_raw = projected[:, :, query_width + key_width :]
    query_rot = rotate(query, positions).astype(jnp.bfloat16)
    key_rot = rotate(key_raw, positions).astype(jnp.bfloat16)
    value_rows = value_raw.astype(jnp.bfloat16)
    cache = jnp.stack(
        [key_rot.reshape(row_count, local_kv * HD), value_rows.reshape(row_count, local_kv * HD)],
        axis=0,
    )[None]
    attended = attend(
        query_rot.reshape(row_count, local_kv, HEADS // KVH, HD), key_rot, value_rows, length
    )
    attended = attended.reshape(row_count, blocks, query_width)
    out_blocks = collect_blocks(w_out, lambda values, bit_index: swapped(values, TENSOR, bit_index))
    partial_sum = jnp.einsum(
        "rkw,kwc->rc",
        attended,
        lax.all_gather(out_blocks, DP, axis=2, tiled=True),
        preferred_element_type=jnp.float32,
    )
    levels_in = TPG.bit_length() - 1
    running = partial_sum
    for bit_index in reversed(range(levels_in)):
        half_rows = running.shape[0] // 2
        upper_half = lax.axis_index(TENSOR) >> bit_index & 1 == 1
        kept = jnp.where(upper_half, running[half_rows:], running[:half_rows]).astype(jnp.bfloat16)
        given = jnp.where(upper_half, running[:half_rows], running[half_rows:]).astype(jnp.bfloat16)
        arrived_sum = swapped(given, TENSOR, bit_index)
        running = kept.astype(jnp.float32) + arrived_sum.astype(jnp.float32)
    hidden = (own_rows.astype(jnp.float32) + running).astype(jnp.bfloat16)
    return (hidden, cache)


def solution(mesh):
    split = Mesh(
        mesh.devices.reshape(4, 2, 2, 2, 4), ("dp_0", "dp_1", "dp_2", "tensor_0", "tensor_1")
    )
    placed = (
        P(DP_TENSOR),
        P(),
        P(DP_TENSOR, None),
        P(),
        P(DP, TENSOR),
        P(DP, TENSOR),
        P(DP, TENSOR),
        P(TENSOR, DP),
    )
    return jax.shard_map(
        shards,
        mesh=split,
        in_specs=placed,
        out_specs=(P(DP_TENSOR, None), P(DP_TENSOR, None, None, None)),
        check_vma=False,
    )
```

profile of v0, /device:TPU:0, one launch (start us, length us, event | category | flops | bytes accessed | tf_op | source)
XLA Modules:
  0.0 527.1 jit_solution(4063840537244072791)
XLA Ops:
  11.6 9.1 %collective-permute-done = bf16[1,256,768]{2,1,0:T(8,128)(2,1)S(1)} collective-permute-done((bf16[1,256,768]{2,1,0:T(8,128)(2,1)S(1)}, bf16[1,256,768]{2,1,0:T(8,128)(2,1)S(1)}, u32[]{:S(2)}, u32[]{:S(2)}) %collective-permute-start) | collective-permute-done | bytes 393248 | tf_op jit(solution)/shard_map/ppermute | solution.py:62
  31.7 9.9 %all-reduce = s32[96]{0:T(128)S(1)} all-reduce(s32[96]{0:T(128)S(1)} %get-tuple-element.44), channel_id=2, replica_groups=mesh['dp_0'=4,'dp_1'=2,'dp_2'=2,'tensor_0'=2,'tensor_1'=4] {'dp_0'}, use_global_device_ids=true, to_apply=%add | all-reduce | flops 96 | bytes 768
  41.7 11.3 %all-gather.5 = s32[4,4,24]{2,1,0:T(4,128)S(1)} all-gather(s32[1,4,24]{2,1,0:T(4,128)S(1)} %reshape.312), channel_id=1, replica_groups=mesh['dp_0'=4,'dp_1'=2,'dp_2'=2,'tensor_0'=2,'tensor_1'=4] {'tensor_1'}, dimensions={0}, use_global_device_ids=true | all-gather | bytes 1920 | tf_op jit(solution)/shard_map/all_gather | solution.py:30
  53.0 6.2 %all_gather.83 = s32[32,24]{1,0:T(8,128)S(1)} all-gather(s32[16,24]{1,0:T(8,128)S(1)} %bitcast.153), channel_id=1, replica_groups=mesh['dp_0'=4,'dp_1'=2,'dp_2'=2,'tensor_0'=2,'tensor_1'=4] {'tensor_0'}, dimensions={0}, use_global_device_ids=true | all-gather | bytes 4608 | tf_op jit(solution)/shard_map/all_gather | solution.py:30
  61.2 4.7 all-gather.7
  66.0 6.0 %all-reduce.3 = s32[48]{0:T(128)S(1)} all-reduce(s32[48]{0:T(128)S(1)} %get-tuple-element.43), channel_id=5, replica_groups=mesh['dp_0'=4,'dp_1'=2,'dp_2'=2,'tensor_0'=2,'tensor_1'=4] {'tensor_0'}, use_global_device_ids=true, to_apply=%add.3 | all-reduce | flops 48 | bytes 384
  73.9 4.5 all-gather.15
  78.4 12.0 %all_gather.99 = s32[32,24]{1,0:T(8,128)S(1)} all-gather(s32[8,24]{1,0:T(8,128)S(1)} %bitcast.156), channel_id=1, replica_groups=mesh['dp_0'=4,'dp_1'=2,'dp_2'=2,'tensor_0'=2,'tensor_1'=4] {'dp_0'}, dimensions={0}, use_global_device_ids=true | all-gather | bytes 3840 | tf_op jit(solution)/shard_map/all_gather | solution.py:30
  90.5 11.9 %all-gather.16 = s32[4,32,24]{1,2,0:T(8,128)S(1)} all-gather(s32[1,32,24]{1,2,0:T(8,128)S(1)} %copy.129), channel_id=1, replica_groups=mesh['dp_0'=4,'dp_1'=2,'dp_2'=2,'tensor_0'=2,'tensor_1'=4] {'tensor_1'}, dimensions={0}, use_global_device_ids=true | all-gather | bytes 15360 | tf_op jit(solution)/shard_map/all_gather | solution.py:30
  106.9 7.7 %all-gather.8 = s32[4,2,24]{2,1,0:T(2,128)S(1)} all-gather(s32[1,2,24]{2,1,0:T(2,128)S(1)} %reshape.318), channel_id=1, replica_groups=mesh['dp_0'=4,'dp_1'=2,'dp_2'=2,'tensor_0'=2,'tensor_1'=4] {'dp_0'}, dimensions={0}, use_global_device_ids=true | all-gather | bytes 960 | tf_op jit(solution)/shard_map/all_gather | solution.py:30
  114.6 12.0 %all_gather.88 = s32[32,24]{1,0:T(8,128)S(1)} all-gather(s32[8,24]{1,0:T(8,128)S(1)} %bitcast.155), channel_id=1, replica_groups=mesh['dp_0'=4,'dp_1'=2,'dp_2'=2,'tensor_0'=2,'tensor_1'=4] {'tensor_1'}, dimensions={0}, use_global_device_ids=true | all-gather | bytes 3840 | tf_op jit(solution)/shard_map/all_gather | solution.py:30
  126.7 5.9 %all-gather.9 = s32[2,32,24]{1,2,0:T(8,128)S(1)} all-gather(s32[1,32,24]{1,2,0:T(8,128)S(1)} %copy.122), channel_id=1, replica_groups=mesh['dp_0'=4,'dp_1'=2,'dp_2'=2,'tensor_0'=2,'tensor_1'=4] {'tensor_0'}, dimensions={0}, use_global_device_ids=true | all-gather | bytes 9216 | tf_op jit(solution)/shard_map/all_gather | solution.py:30
  140.8 10.4 %all-gather.12 = s32[4,4,24]{2,1,0:T(4,128)S(1)} all-gather(s32[1,4,24]{2,1,0:T(4,128)S(1)} %bitcast.159), channel_id=1, replica_groups=mesh['dp_0'=4,'dp_1'=2,'dp_2'=2,'tensor_0'=2,'tensor_1'=4] {'dp_0'}, dimensions={0}, use_global_device_ids=true | all-gather | bytes 1920 | tf_op jit(solution)/shard_map/all_gather | solution.py:30
  151.2 11.9 %all_gather.94 = s32[64,24]{1,0:T(8,128)S(1)} all-gather(s32[16,24]{1,0:T(8,128)S(1)} %bitcast.154), channel_id=1, replica_groups=mesh['dp_0'=4,'dp_1'=2,'dp_2'=2,'tensor_0'=2,'tensor_1'=4] {'tensor_1'}, dimensions={0}, use_global_device_ids=true | all-gather | bytes 7680 | tf_op jit(solution)/shard_map/all_gather | solution.py:30
  163.2 5.9 %all-gather.13 = s32[2,64,24]{1,2,0:T(8,128)S(1)} all-gather(s32[1,64,24]{1,2,0:T(8,128)S(1)} %copy.126), channel_id=1, replica_groups=mesh['dp_0'=4,'dp_1'=2,'dp_2'=2,'tensor_0'=2,'tensor_1'=4] {'tensor_0'}, dimensions={0}, use_global_device_ids=true | all-gather | bytes 18432 | tf_op jit(solution)/shard_map/all_gather | solution.py:30
  170.6 7.3 %all-reduce.4 = s32[128]{0:T(128)S(1)} all-reduce(s32[128]{0:T(128)S(1)} %slice_dynamic-update-slice_fusion), channel_id=6, replica_groups=mesh['dp_0'=4,'dp_1'=2,'dp_2'=2,'tensor_0'=2,'tensor_1'=4] {'tensor_1'}, use_global_device_ids=true, to_apply=%add.4 | all-reduce | flops 128 | bytes 1024
  178.0 5.9 %all-gather.17 = s32[2,4,32]{2,1,0:T(4,128)S(1)} all-gather(s32[1,4,32]{2,1,0:T(4,128)S(1)} %reshape.336), channel_id=1, replica_groups=mesh['dp_0'=4,'dp_1'=2,'dp_2'=2,'tensor_0'=2,'tensor_1'=4] {'tensor_0'}, dimensions={0}, use_global_device_ids=true | all-gather | bytes 1536 | tf_op jit(solution)/shard_map/all_gather | solution.py:30
  185.7 4.4 all_gather.104
  190.0 11.9 %all_gather.105 = s32[128,32]{1,0:T(8,128)S(1)} all-gather(s32[32,32]{1,0:T(8,128)S(1)} %all_gather.104), channel_id=1, replica_groups=mesh['dp_0'=4,'dp_1'=2,'dp_2'=2,'tensor_0'=2,'tensor_1'=4] {'dp_0'}, dimensions={0}, use_global_device_ids=true | all-gather | bytes 20480 | tf_op jit(solution)/shard_map/all_gather | solution.py:30
  203.3 24.9 %copy.132 = bf16[128256,32]{1,0:T(8,128)(2,1)} copy(bf16[128256,32]{0,1:T(8,128)(2,1)} %bitcast.131) | data formatting | bytes 16416768 | tf_op jit(solution)/shard_map/transpose | solution.py:126
  228.2 37.7 %reshape.279 = bf16[32064,128]{1,0:T(8,128)(2,1)} reshape(bf16[128256,32]{1,0:T(8,128)(2,1)} %copy.132) | data formatting | bytes 16416768 | tf_op jit(solution)/shard_map/reshape | solution.py:126
  265.9 59.3 %gather_fusion = bf16[16384,128]{1,0:T(8,128)(2,1)} fusion(bf16[32064,128]{1,0:T(8,128)(2,1)} %reshape.279, s32[16384]{0:T(1024)S(1)} %broadcast_clamp_fusion), kind=kCustom, calls=%fused_computation | custom fusion | bytes 8454144 | tf_op jit(solution)/shard_map/jit(_take)/gather | solution.py:127
  325.2 6.5 %copy.133 = bf16[16384,128]{0,1:T(8,128)(2,1)} copy(bf16[16384,128]{1,0:T(8,128)(2,1)} %gather_fusion) | data formatting | bytes 8388608 | tf_op jit(solution)/shard_map/jit(_take)/gather | solution.py:127
  331.8 4.5 select_reduce_fusion
  338.9 6.1 %all-to-all-start = ((bf16[128,512,32]{1,2,0:T(8,128)(2,1)}), bf16[128,512,32]{1,2,0:T(8,128)(2,1)}, u32[]{:S(2)}, u32[]{:S(2)}) async-start(bf16[128,512,32]{1,2,0:T(8,128)(2,1)} %bitcast.128), calls=%async_computation | async-start | bytes 8388608 | tf_op jit(solution)/shard_map/all_to_all | solution.py:153
  349.4 47.5 %all-to-all-done = bf16[128,512,32]{1,2,0:T(8,128)(2,1)} async-done(((bf16[128,512,32]{1,2,0:T(8,128)(2,1)}), bf16[128,512,32]{1,2,0:T(8,128)(2,1)}, u32[]{:S(2)}, u32[]{:S(2)}) %all-to-all-start) | async-done | bytes 4194336 | tf_op jit(solution)/shard_map/all_to_all | solution.py:153
  400.1 11.9 %fusion.3 = f32[512,2,768]{2,0,1:T(8,128)S(1)} fusion(bf16[2,4096,768]{2,1,0:T(8,128)(2,1)} %all-gather.21.cloned.1.call-done, bf16[512,4096]{0,1:T(8,128)(2,1)} %bitcast.36, f32[4096]{0:T(1024)S(1)} %copy-done.6, f32[512]{0:T(512)S(1)} %add_rsqrt_fusion), kind=kOutput, calls=%fused_computation.10 | convolution fusion | flops 6450839552 | bytes 19941376 | tf_op jit(solution)/shard_map/rd,kdc->rkc/dot_general | solution.py:167
  421.7 5.7 %fusion.25 = (f32[2,4,512]{2,1,0:T(4,128)S(1)}, f32[2,4,512,512]{2,3,1,0:T(8,128)}) fusion(f32[2,512,512,4]{2,1,3,0:T(8,128)S(1)} %fusion.12, pred[512,512]{0,1:T(8,128)(4,1)S(1)} %copy-done.3), kind=kOutput, calls=%fused_computation.82 | output fusion | flops 12583423 | bytes 17055744 | tf_op jit(solution)/shard_map/while/body/eval_jaxpr/sub | solution.py:91
  427.4 4.4 fusion.11
  431.9 8.4 %convolution_bitcast_fusion = bf16[512,4096]{1,0:T(8,128)(2,1)S(1)} fusion(bf16[512,2,512]{0,2,1:T(8,128)(2,1)S(1)} %bitcast.160, bf16[2,512,4096]{2,1,0:T(8,128)(2,1)} %all-gather.23.cloned.1.call-done), kind=kOutput, calls=%fused_computation.7 | convolution fusion | flops 4294967296 | bytes 13631488 | tf_op jit(solution)/shard_map/rkw,kwc->rc/dot_general | solution.py:192
  443.0 46.5 %collective-permute-done.2 = bf16[256,4096]{1,0:T(8,128)(2,1)} collective-permute-done((bf16[256,4096]{1,0:T(8,128)(2,1)S(1)}, bf16[256,4096]{1,0:T(8,128)(2,1)}, u32[]{:S(2)}, u32[]{:S(2)}) %collective-permute-start.2) | collective-permute-done | bytes 2097184 | tf_op jit(solution)/shard_map/ppermute | solution.py:62
  505.1 12.2 %collective-permute-done.3 = bf16[128,4096]{1,0:T(8,128)(2,1)} collective-permute-done((bf16[128,4096]{1,0:T(8,128)(2,1)}, bf16[128,4096]{1,0:T(8,128)(2,1)}, u32[]{:S(2)}, u32[]{:S(2)}) %collective-permute-start.3) | collective-permute-done | bytes 1048608 | tf_op jit(solution)/shard_map/ppermute | solution.py:62
  (121 shorter events, 74.9 us)
Async XLA Ops:
  7.2 19.1 %copy-start.12 = (u32[128]{0:T(128)S(1)}, u32[128]{0:T(128)}, u32[]{:S(2)}) copy-start(u32[128]{0:T(128)} %constant.129) | copy-start | bytes 1540
  7.2 19.7 %copy-start.11 = (u32[128]{0:T(128)S(1)}, u32[128]{0:T(128)}, u32[]{:S(2)}) copy-start(u32[128]{0:T(128)} %constant.144) | copy-start | bytes 1540
  7.2 21.5 %copy-start.10 = (u32[128]{0:T(128)S(1)}, u32[128]{0:T(128)}, u32[]{:S(2)}) copy-start(u32[128]{0:T(128)} %constant.134) | copy-start | bytes 1540
  7.2 22.8 %copy-start.9 = (u32[128]{0:T(128)S(1)}, u32[128]{0:T(128)}, u32[]{:S(2)}) copy-start(u32[128]{0:T(128)} %constant.139) | copy-start | bytes 1540
  7.2 162.0 %copy-start.8 = (u32[128]{0:T(128)S(1)}, u32[128]{0:T(128)}, u32[]{:S(2)}) copy-start(u32[128]{0:T(128)} %constant.149) | copy-start | bytes 1540
  7.2 15.7 %copy-start.4 = (bf16[512,256]{1,0:T(8,128)(2,1)S(1)}, bf16[512,256]{1,0:T(8,128)(2,1)}, u32[]{:S(2)}) copy-start(bf16[512,256]{1,0:T(8,128)(2,1)} %param.15) | copy-start | bytes 786436
  7.2 24.0 %copy-start.5 = (s32[128]{0:T(128)S(1)}, s32[128]{0:T(128)}, u32[]{:S(2)}) copy-start(s32[128]{0:T(128)} %param.8) | copy-start | bytes 1540
  7.2 392.8 %all-gather.21.cloned.1.call-start = ((), (), s32[]{:S(2)}) async-start(), calls=%async_computation.1 | async-start | bytes 13369344 | tf_op jit(solution)/shard_map/all_gather | solution.py:170
  8.4 12.3 %collective-permute-start = (bf16[1,256,768]{2,1,0:T(8,128)(2,1)S(1)}, bf16[1,256,768]{2,1,0:T(8,128)(2,1)S(1)}, u32[]{:S(2)}, u32[]{:S(2)}) collective-permute-start(bf16[1,256,768]{2,1,0:T(8,128)(2,1)S(1)} %maximum_bitcast_fusion.1), channel_id=1, source_target_pairs={{0,4},{4,0},{1,5},{5,1},{2,6},{6,2},{3,7},{7,3},{8,12},{12,8},{9,1... | collective-permute-start | bytes 1179656 | tf_op jit(solution)/shard_map/ppermute | solution.py:62
  22.9 409.0 %all-gather.23.cloned.1.call-start = ((), (), s32[]{:S(2)}) async-start(), calls=%async_computation.2 | async-start | bytes 8912896 | tf_op jit(solution)/shard_map/all_gather | solution.py:195
  23.0 179.1 %collective-permute-start.1 = (bf16[1,512,256]{2,1,0:T(8,128)(2,1)S(1)}, bf16[1,512,256]{2,1,0:T(8,128)(2,1)S(1)}, u32[]{:S(2)}, u32[]{:S(2)}) collective-permute-start(bf16[1,512,256]{2,1,0:T(8,128)(2,1)S(1)} %bitcast.148), channel_id=1, source_target_pairs={{0,4},{4,0},{1,5},{5,1},{2,6},{6,2},{3,7},{7,3},{8,12},{12,8},{9,1... | collective-permute-start | bytes 786440 | tf_op jit(solution)/shard_map/ppermute | solution.py:62
  338.9 8.4 %copy-start.7 = (s32[32]{0:T(128)S(1)}, s32[32]{0:T(128)}, u32[]{:S(2)}) copy-start(s32[32]{0:T(128)} %param.9) | copy-start | bytes 388
  338.9 58.0 %all-to-all-start = ((bf16[128,512,32]{1,2,0:T(8,128)(2,1)}), bf16[128,512,32]{1,2,0:T(8,128)(2,1)}, u32[]{:S(2)}, u32[]{:S(2)}) async-start(bf16[128,512,32]{1,2,0:T(8,128)(2,1)} %bitcast.128), calls=%async_computation | async-start | bytes 8388608 | tf_op jit(solution)/shard_map/all_to_all | solution.py:153
  345.1 55.0 %copy-start.6 = (f32[4096]{0:T(1024)S(1)}, f32[4096]{0:T(1024)}, u32[]{:S(2)}) copy-start(f32[4096]{0:T(1024)} %param.11) | copy-start | bytes 49156
  412.0 1.6 copy-start.2
  420.3 1.4 copy-start.3
  440.3 1.9 copy-start
  442.4 47.1 %collective-permute-start.2 = (bf16[256,4096]{1,0:T(8,128)(2,1)S(1)}, bf16[256,4096]{1,0:T(8,128)(2,1)}, u32[]{:S(2)}, u32[]{:S(2)}) collective-permute-start(bf16[256,4096]{1,0:T(8,128)(2,1)S(1)} %select_convert_fusion), channel_id=1, source_target_pairs={{0,2},{2,0},{1,3},{3,1},{4,6},{6,4},{5,7},{7,5},{8,10},{10,8},{9,1... | collective-permute-start | bytes 6291464 | tf_op jit(solution)/shard_map/ppermute | solution.py:62
  494.5 22.9 %collective-permute-start.3 = (bf16[128,4096]{1,0:T(8,128)(2,1)}, bf16[128,4096]{1,0:T(8,128)(2,1)}, u32[]{:S(2)}, u32[]{:S(2)}) collective-permute-start(bf16[128,4096]{1,0:T(8,128)(2,1)} %select_convert_fusion.2), channel_id=1, source_target_pairs={{0,1},{1,0},{2,3},{3,2},{4,5},{5,4},{6,7},{7,6},{8,9},{9,8},{10,11... | collective-permute-start | bytes 3145736 | tf_op jit(solution)/shard_map/ppermute | solution.py:62
  498.5 18.9 %copy-start.1 = (bf16[128,4096]{1,0:T(8,128)(2,1)S(1)}, bf16[128,4096]{1,0:T(8,128)(2,1)}, u32[]{:S(2)}) copy-start(bf16[128,4096]{1,0:T(8,128)(2,1)} %copy.156) | copy-start | bytes 3145732
Sparse Core Ops, SparseCore 0:
  23.0 74.8 all-gather.20
  203.1 57.8 all-gather.22
where the time goes:
time: 532 us; the launch traced here: 527 us
  blocking collectives  167 us (31%)
  local copies, waits for them, and re-layouts  154 us (29%)
  waiting for transfers between devices  115 us (22%)
  other arithmetic  32.1 us (6%)
  matrix products  26.1 us (5%)
  between operations  17.6 us (3%)
  starting transfers between devices  14.7 us (3%)
    all_gather x20, blocking collectives, stacked_from(): pieces = lax.all_gather(pieces, axes[k], axis=0, tiled=True)  138 us
    ppermute x4, waiting for transfers between devices, swapped(): return lax.ppermute(block, axis, route)  67.9 us
    gather x2, local copies, waits for them, and re-layouts, lookup_rows(): jnp.take(token_major, token_ids // packing, axis=0)  65.8 us
    all_to_all x1, waiting for transfers between devices, shards(): lax.all_to_all(outgoing.reshape(devices, row_count, columns), DP_TENSOR,...  47.5 us
    reshape x1, local copies, waits for them, and re-layouts, lookup_rows(): embed_table.T.reshape(vocab_size // packing, packing * columns)  37.7 us
    unnamed x5, blocking collectives  29.4 us
    transpose x1, local copies, waits for them, and re-layouts, lookup_rows(): embed_table.T.reshape(vocab_size // packing, packing * columns)  24.9 us
    dot_general x1, matrix products, shards(): jnp.einsum('rd,kdc->rkc', normed, lax.all_gather(stacked, DP, axis=1, til...  11.9 us
  transfers between devices with their start and end apart: 7, of which 4 were waited for; matrix products, arithmetic and copies ran while one was open for 36% of the time, Pallas kernels for 0%

commit v1 on v0

v1 whole, which is shorter than its diff:
```python
import jax
import jax.numpy as jnp
from jax import lax
from jax.experimental import pallas as pl
from jax.experimental.pallas import tpu as pltpu
from jax.sharding import Mesh
from jax.sharding import PartitionSpec as P

HEADS = 32
KVH = 8
HD = 128
TPG = 4
AXES = ("z", "xlo", "core", "xhi", "y")
DP = ("z", "xlo", "core")
TENSOR = ("xhi", "y")

norm_eps = 1e-05
rope_theta = 500000.0

BLOCKS = 252
STRIP = BLOCKS * 128


def lookup_kernel(row_ref, strip_ref, table_ref, out_ref, raw, major, rows, sems):
    feats, vocab = table_ref.shape
    tiles = vocab // 128
    count = sems.shape[0]
    ends = [tiles * k // count for k in range(count + 1)]
    copies = []
    for k in range(count):
        part = pl.ds(ends[k] * 128, (ends[k + 1] - ends[k]) * 128)
        copies.append(pltpu.make_async_copy(table_ref.at[:, part], raw.at[:, part], sems.at[k]))
    for copy in copies:
        copy.start()
    for copy in copies:
        copy.wait()

    def turn(b, _):
        parts = []
        for strip in range(4):
            first = jnp.minimum(b * 128 + strip * STRIP, vocab - 128)
            parts.append(raw[:, pl.ds(pl.multiple_of(first, 128), 128)])
        block = jnp.concatenate(parts, axis=0)
        major[pl.ds(pl.multiple_of(b * 128, 128), 128), :] = block.T.astype(jnp.float32)
        return 0

    lax.fori_loop(0, BLOCKS, turn, 0, unroll=12)
    eye = (
        lax.broadcasted_iota(jnp.int32, (128, 128), 0)
        == lax.broadcasted_iota(jnp.int32, (128, 128), 1)
    ).astype(jnp.bfloat16)
    prompt = rows.shape[0]

    def group(g, _):
        def some(s, _):
            for i in range(128):
                rows[pl.ds(s * 128 + i, 1), :] = major[pl.ds(row_ref[g * prompt + s * 128 + i], 1), :]
            return 0

        lax.fori_loop(0, prompt // 128, some, 0)
        found = lax.dot_general(
            eye,
            rows[...].astype(jnp.bfloat16),
            (((1,), (1,)), ((), ())),
            preferred_element_type=jnp.float32,
        )
        strip = strip_ref[pl.ds(g, 1), :]
        chosen = found[:feats]
        for k in range(1, 4):
            chosen = jnp.where(strip == k, found[k * feats : (k + 1) * feats], chosen)
        out_ref[pl.ds(g, 1)] = chosen.astype(jnp.bfloat16)[None]
        return 0

    lax.fori_loop(0, out_ref.shape[0], group, 0)


def lookup(table, ids, prompt):
    feats, vocab = table.shape
    groups = ids.shape[0] // prompt
    strip = ids // STRIP
    row = ids - strip * STRIP
    return pl.pallas_call(
        lookup_kernel,
        out_shape=jax.ShapeDtypeStruct((groups, feats, prompt), jnp.bfloat16),
        in_specs=[
            pl.BlockSpec(memory_space=pltpu.SMEM),
            pl.BlockSpec(memory_space=pltpu.VMEM),
            pl.BlockSpec(memory_space=pl.ANY),
        ],
        out_specs=pl.BlockSpec(memory_space=pltpu.VMEM),
        scratch_shapes=[
            pltpu.VMEM((feats, vocab), jnp.bfloat16),
            pltpu.VMEM((STRIP, 128), jnp.float32),
            pltpu.VMEM((prompt, 128), jnp.float32),
            pltpu.SemaphoreType.DMA((6,)),
        ],
        compiler_params=pltpu.CompilerParams(vmem_limit_bytes=50 * 2**20),
        cost_estimate=pl.CostEstimate(flops=30_000_000_000, bytes_accessed=8_000_000, transcendentals=0),
    )(row, strip.reshape(groups, prompt), table)


def rotate(heads_in, positions):
    half = heads_in.shape[-1] // 2
    freq = rope_theta ** (-2.0 * jnp.arange(half, dtype=jnp.float32) / heads_in.shape[-1])
    angle = positions.astype(jnp.float32)[:, None] * freq[None, :]
    cosine = jnp.cos(angle)[:, None, :]
    sine = jnp.sin(angle)[:, None, :]
    first = heads_in[..., :half]
    second = heads_in[..., half:]
    return jnp.concatenate(
        [first * cosine - second * sine, second * cosine + first * sine], axis=-1
    )


def attend(query_rot, key_rot, value_rows, length):
    row_count = query_rot.shape[0]
    positions = jnp.arange(row_count, dtype=jnp.int32)
    scores = jnp.einsum(
        "qhgd,khd->hgqk", query_rot, key_rot, preferred_element_type=jnp.float32
    ) / jnp.sqrt(jnp.float32(HD))
    allowed = (positions[None, :] <= positions[:, None]) & (positions[None, :] < length)
    scores = jnp.where(allowed, scores, -1e30)
    biggest = jnp.max(scores, axis=-1, keepdims=True)
    expd = jnp.exp(scores - biggest)
    weights = (expd / jnp.sum(expd, axis=-1, keepdims=True)).astype(jnp.bfloat16)
    result = jnp.einsum("hgqk,khd->qhgd", weights, value_rows, preferred_element_type=jnp.float32)
    return result.astype(jnp.bfloat16).reshape(row_count, -1)


def swapped(block, apart):
    return lax.ppermute(block, "y", [(k, k ^ 1 << apart) for k in range(TPG)])


def shards(prompt_ids, prompt_lengths, embed_table, norm_gain, w_query, w_key, w_value, w_out):
    quarter = prompt_ids.shape[0]
    row_count = quarter * TPG
    devices = lax.axis_size(AXES)
    features = embed_table.shape[0]
    model_width = features * devices
    member = lax.axis_index("y")
    group_index = lax.axis_index(("z", "xlo", "core", "xhi"))
    length = lax.dynamic_slice_in_dim(prompt_lengths, group_index, 1, 0)[0]
    all_ids = lax.all_gather(prompt_ids, AXES, axis=0, tiled=True)

    query_width = w_query.shape[1]
    key_width = w_key.shape[1]
    packed = jnp.concatenate([w_query, w_key, w_value], axis=1)
    wide = lax.all_gather(packed, ("xhi", "z", "xlo", "core"), axis=0, tiled=True)
    wide = wide.reshape(2, model_width, packed.shape[1])
    out_parts = lax.all_gather(w_out, ("xhi", "z", "xlo", "core"), axis=0, tiled=False)

    picked = lookup(embed_table, all_ids, row_count)
    group_count = devices // TPG
    outgoing = jnp.broadcast_to(
        picked[:, None], (group_count, TPG, features, row_count)
    ).reshape(devices, features, row_count)
    arrived = lax.all_to_all(outgoing, AXES, split_axis=0, concat_axis=0, tiled=True)
    tokens = arrived.reshape(model_width, row_count)
    wide_in = tokens.astype(jnp.float32)
    scale = lax.rsqrt(jnp.mean(wide_in * wide_in, axis=0, keepdims=True) + norm_eps)
    normed = (wide_in * scale * norm_gain[:, None]).astype(jnp.bfloat16)
    own_rows = lax.dynamic_slice_in_dim(tokens, member * quarter, quarter, 1).T

    projected = jnp.einsum("dr,kdc->rkc", normed, wide, preferred_element_type=jnp.float32)
    blocks = projected.shape[1]
    local_heads = blocks * query_width // HD
    local_kv = blocks * key_width // HD
    positions = jnp.arange(row_count, dtype=jnp.int32)
    query = projected[:, :, :query_width].reshape(row_count, local_heads, HD)
    key_raw = projected[:, :, query_width : query_width + key_width]
    value_rows = projected[:, :, query_width + key_width :].astype(jnp.bfloat16)
    query_rot = rotate(query, positions).astype(jnp.bfloat16)
    key_rot = rotate(key_raw, positions).astype(jnp.bfloat16)
    cache = jnp.stack(
        [key_rot.reshape(row_count, local_kv * HD), value_rows.reshape(row_count, local_kv * HD)],
        axis=0,
    )[None]
    attended = attend(
        query_rot.reshape(row_count, local_kv, HEADS // KVH, HD), key_rot, value_rows, length
    )
    attended = attended.reshape(row_count, blocks, query_width)
    out_wide = out_parts.reshape(blocks, -1, query_width, out_parts.shape[-1])
    partial_sum = jnp.einsum(
        "rkw,kdwc->rdc", attended, out_wide, preferred_element_type=jnp.float32
    ).reshape(row_count, model_width)
    running = partial_sum
    for bit_index in reversed(range(2)):
        half_rows = running.shape[0] // 2
        upper_half = member >> bit_index & 1 == 1
        kept = jnp.where(upper_half, running[half_rows:], running[:half_rows]).astype(jnp.bfloat16)
        given = jnp.where(upper_half, running[:half_rows], running[half_rows:]).astype(jnp.bfloat16)
        arrived_sum = swapped(given, bit_index)
        running = kept.astype(jnp.float32) + arrived_sum.astype(jnp.float32)
    hidden = (own_rows.astype(jnp.float32) + running).astype(jnp.bfloat16)
    return (hidden, cache)


def solution(mesh):
    split = Mesh(mesh.devices.reshape(4, 2, 2, 2, 4), AXES)
    placed = (
        P(AXES),
        P(),
        P(AXES, None),
        P(),
        P(DP, TENSOR),
        P(DP, TENSOR),
        P(DP, TENSOR),
        P(TENSOR, DP),
    )
    return jax.shard_map(
        shards,
        mesh=split,
        in_specs=placed,
        out_specs=(P(AXES, None), P(AXES, None, None, None)),
        check_vma=False,
    )
```

time: 532 us -> 556 us (1.045)
  blocking collectives: 167 us -> 319 us
  local copies, waits for them, and re-layouts: 154 us -> 16.1 us
  Pallas kernels: 0 us -> 28.1 us
  starting transfers between devices: 14.7 us -> 7.89 us
    all_gather x20 -> x1, blocking collectives: 138 us -> 319 us  [shards(): all_ids = lax.all_gather(prompt_ids, AXES, axis=0, tiled=True)]
    gather x2 -> x0, local copies, waits for them, and re-layouts: 65.8 us -> none  [lookup_rows(): jnp.take(token_major, token_ids // packing, axis=0)]
    reshape x1, local copies, waits for them, and re-layouts: 37.7 us -> 0.01 us  [lookup(): strip.reshape(groups, prompt)]
    unnamed x5 -> x0, blocking collectives: 29.4 us -> none
    pallas_call x0 -> x1, Pallas kernels: none -> 28.1 us  [lookup(): pl.pallas_call(lookup_kernel, out_shape=jax.ShapeDtypeStruct((groups, fea...]
    transpose x5 -> x0, local copies, waits for them, and re-layouts: 25 us -> none  [the longest x1 24.9 us: lookup_rows(): embed_table.T.reshape(vocab_size // packing, packing * columns)]
    ppermute x4 -> x2, starting transfers between devices: 8.45 us -> 1.84 us  [swapped(): return lax.ppermute(block, 'y', [(k, k ^ 1 << apart) for k in range(TPG)])]
    convert_element_type x0 -> x2, other arithmetic: none -> 6.32 us  [the longest x1 4.09 us: shards(): normed = (wide_in * scale * norm_gain[:, None]).astype(jnp.bfloat16)]
  transfers between devices with their start and end apart: 7 -> 5, of which waited for: 4 -> 3; matrix products, arithmetic and copies ran while one was open for 36% -> 8% of each run, Pallas kernels for 0% -> 5%
where the time goes in v1:
time: 556 us; the launch traced here: 553 us
  blocking collectives  319 us (57%)
  waiting for transfers between devices  114 us (21%)
  Pallas kernels  28.1 us (5%)
  other arithmetic  27.1 us (5%)
  matrix products  27 us (5%)
  local copies, waits for them, and re-layouts  16.1 us (3%)
  between operations  14.2 us (3%)
  starting transfers between devices  7.89 us (1%)
    all_gather x1, blocking collectives, shards(): all_ids = lax.all_gather(prompt_ids, AXES, axis=0, tiled=True)  319 us
    ppermute x2, waiting for transfers between devices, swapped(): return lax.ppermute(block, 'y', [(k, k ^ 1 << apart) for k in range(TPG)])  65.9 us
    all_to_all x1, waiting for transfers between devices, shards(): lax.all_to_all(outgoing, AXES, split_axis=0, concat_axis=0, tiled=True)  47.7 us
    pallas_call x1, Pallas kernels, lookup(): pl.pallas_call(lookup_kernel, out_shape=jax.ShapeDtypeStruct((groups, fea...  28.1 us
  transfers between devices with their start and end apart: 5, of which 3 were waited for; matrix products, arithmetic and copies ran while one was open for 8% of the time, Pallas kernels for 5%

profile of v1, /device:TPU:0, one launch (start us, length us, event | category | flops | bytes accessed | tf_op | source)
XLA Modules:
  0.0 553.3 jit_solution(15470499420258106733)
XLA Ops:
  7.2 1.8 pad_maximum_fusion
  9.1 0.7 all-gather.7.cloned.1.call-update
  9.8 318.6 %all-gather.1 = s32[128,1,128]{2,1,0:T(1,128)S(1)} all-gather(s32[1,1,128]{2,1,0:T(1,128)} %bitcast.70), channel_id=1, replica_groups=mesh['z'=4,'xlo'=2,'core'=2,'xhi'=2,'y'=4] {'z','xlo','core','xhi','y'}, dimensions={0}, use_global_device_ids=true | all-gather | bytes 66048 | tf_op jit(solution)/shard_map/all_gather | solution.py:143
  328.4 28.1 %shard_map.95 = bf16[32,32,512]{2,1,0:T(8,128)(2,1)S(1)} custom-call(s32[16384]{0:T(1024)S(1)} %get-tuple-element.15.row_ref, s32[32,512]{1,0:T(8,128)S(1)} %reshape.133.strip_ref, bf16[32,128256]{1,0:T(8,128)(2,1)} %table_ref.1), custom_call_target="tpu_custom_call" | custom-call | flops 30000001024 | bytes 8000000 | tf_op jit(solution)/shard_map/pallas_call | solution.py:82
  356.5 2.5 broadcast_in_dim.10
  359.0 6.0 %all-to-all-start = ((bf16[128,32,512]{2,1,0:T(8,128)(2,1)}), bf16[128,32,512]{2,1,0:T(8,128)(2,1)}, u32[]{:S(2)}, u32[]{:S(2)}) async-start(bf16[128,32,512]{2,1,0:T(8,128)(2,1)} %bitcast.62), calls=%async_computation | async-start | bytes 8388608 | tf_op jit(solution)/shard_map/all_to_all | solution.py:157
  365.7 0.8 copy.45
  366.5 0.8 copy.46
  368.5 0.8 fusion.15
  369.4 47.7 %all-to-all-done = bf16[128,32,512]{2,1,0:T(8,128)(2,1)} async-done(((bf16[128,32,512]{2,1,0:T(8,128)(2,1)}), bf16[128,32,512]{2,1,0:T(8,128)(2,1)}, u32[]{:S(2)}, u32[]{:S(2)}) %all-to-all-start) | async-done | bytes 4194336 | tf_op jit(solution)/shard_map/all_to_all | solution.py:157
  417.0 3.1 fusion.1
  420.2 4.1 fusion.3
  424.3 10.7 %fusion.24 = f32[512,2,768]{2,0,1:T(8,128)S(1)} fusion(bf16[4096,512,1]{1,0,2:T(8,128)(2,1)} %bitcast.64, bf16[2,4096,768]{2,1,0:T(8,128)(2,1)} %bitcast.71), kind=kOutput, calls=%fused_computation.55 | convolution fusion | flops 6442450944 | bytes 19922944 | tf_op jit(solution)/shard_map/dr,kdc->rkc/dot_general | solution.py:164
  435.0 1.7 copy-done
  436.7 1.7 slice.53
  438.3 1.9 copy.47
  441.6 1.6 multiply_subtract_fusion
  443.4 1.3 fusion.11
  444.8 5.7 %fusion.22 = (f32[2,4,512]{2,1,0:T(4,128)S(1)}, f32[2,4,512,512]{2,3,1,0:T(8,128)}) fusion(f32[2,512,512,4]{2,1,3,0:T(8,128)S(1)} %fusion.11, pred[512,512]{0,1:T(8,128)(4,1)S(1)} %copy-done.2), kind=kOutput, calls=%fused_computation.53 | output fusion | flops 12583423 | bytes 17055744 | tf_op jit(solution)/shard_map/sub | solution.py:124
  450.5 4.4 fusion.10
  454.9 10.5 %convolution_bitcast_fusion = bf16[512,16,256]{0,2,1:T(8,128)(2,1)S(1)} fusion(bf16[512,2,512,1]{0,2,3,1:T(8,128)(2,1)S(1)} %bitcast.73, bf16[2,16,512,256]{3,2,1,0:T(8,128)(2,1)} %bitcast.72), kind=kOutput, calls=%fused_computation.17 | convolution fusion | flops 4294967296 | bytes 13631488 | tf_op jit(solution)/shard_map/rkw,kdwc->rdc/dot_general | solution.py:183
  465.5 2.2 select_convert_fusion.1
  468.2 46.6 %collective-permute-done = bf16[256,4096]{0,1:T(8,128)(2,1)S(1)} collective-permute-done((bf16[256,4096]{0,1:T(8,128)(2,1)}, bf16[256,4096]{0,1:T(8,128)(2,1)S(1)}, u32[]{:S(2)}, u32[]{:S(2)}) %collective-permute-start) | collective-permute-done | bytes 2097184 | tf_op jit(solution)/shard_map/ppermute | solution.py:131
  514.8 1.3 copy-done.1
  516.1 2.8 convert_add_fusion
  518.9 1.1 select_convert_fusion.2
  520.0 1.3 collective-permute-start.1
  521.5 1.1 slice.81
  522.8 1.0 copy.57
  523.8 19.3 %collective-permute-done.1 = bf16[128,4096]{0,1:T(8,128)(2,1)} collective-permute-done((bf16[128,4096]{0,1:T(8,128)(2,1)}, bf16[128,4096]{0,1:T(8,128)(2,1)}, u32[]{:S(2)}, u32[]{:S(2)}) %collective-permute-start.1) | collective-permute-done | bytes 1048608 | tf_op jit(solution)/shard_map/ppermute | solution.py:131
  543.1 2.1 fusion.9
  545.2 1.3 copy.56
  (30 shorter events, 4.3 us)
Async XLA Ops:
  7.2 417.1 %all-gather.5.cloned.1.call-start = ((), (), s32[]{:S(2)}) async-start(), calls=%async_computation.1 | async-start | bytes 12976128 | tf_op jit(solution)/shard_map/all_gather | solution.py:148
  9.0 445.9 %all-gather.7.cloned.1.call-start = ((), (), s32[]{:S(2)}) async-start(), calls=%async_computation.2 | async-start | bytes 8650752 | tf_op jit(solution)/shard_map/all_gather | solution.py:150
  359.0 6.0 %copy-start.3 = (f32[4096]{0:T(1024)S(1)}, f32[4096]{0:T(1024)}, u32[]{:S(2)}) copy-start(f32[4096]{0:T(1024)} %param.11) | copy-start | bytes 49156
  359.0 8.3 %copy-start.4 = (s32[32]{0:T(128)S(1)}, s32[32]{0:T(128)}, u32[]{:S(2)}) copy-start(s32[32]{0:T(128)} %param.9) | copy-start | bytes 388
  359.0 58.0 %all-to-all-start = ((bf16[128,32,512]{2,1,0:T(8,128)(2,1)}), bf16[128,32,512]{2,1,0:T(8,128)(2,1)}, u32[]{:S(2)}, u32[]{:S(2)}) async-start(bf16[128,32,512]{2,1,0:T(8,128)(2,1)} %bitcast.62), calls=%async_computation | async-start | bytes 8388608 | tf_op jit(solution)/shard_map/all_to_all | solution.py:157
  435.0 1.7 copy-start
  443.4 1.4 copy-start.2
  467.7 47.1 %collective-permute-start = (bf16[256,4096]{0,1:T(8,128)(2,1)}, bf16[256,4096]{0,1:T(8,128)(2,1)S(1)}, u32[]{:S(2)}, u32[]{:S(2)}) collective-permute-start(bf16[256,4096]{0,1:T(8,128)(2,1)} %bitcast.23), channel_id=1, source_target_pairs={{0,2},{1,3},{2,0},{3,1},{4,6},{5,7},{6,4},{7,5},{8,10},{9,11},{10,... | collective-permute-start | bytes 6291464 | tf_op jit(solution)/shard_map/ppermute | solution.py:131
  514.8 1.3 copy-start.1
  520.0 23.1 %collective-permute-start.1 = (bf16[128,4096]{0,1:T(8,128)(2,1)}, bf16[128,4096]{0,1:T(8,128)(2,1)}, u32[]{:S(2)}, u32[]{:S(2)}) collective-permute-start(bf16[128,4096]{0,1:T(8,128)(2,1)} %select_convert_fusion.2), channel_id=1, source_target_pairs={{0,1},{1,0},{2,3},{3,2},{4,5},{5,4},{6,7},{7,6},{8,9},{9,8},{10,11... | collective-permute-start | bytes 3145736 | tf_op jit(solution)/shard_map/ppermute | solution.py:131
Sparse Core Ops, SparseCore 0:
  10.3 78.9 all-gather.4
  91.0 66.2 all-gather.6

commit v2 on v1

--- a/solution.py
+++ b/solution.py
@@ -17,21 +17,46 @@
 norm_eps = 1e-05
 rope_theta = 500000.0
 
+MESH = pl.DeviceIdType.MESH
 BLOCKS = 252
 STRIP = BLOCKS * 128
 
-
-def lookup_kernel(row_ref, strip_ref, table_ref, out_ref, raw, major, rows, sems):
+def place(g, y):
+    return (g // 8, g // 4 % 2, g // 2 % 2, g % 2, y)
+
+def front_kernel(ids_ref, table_ref, out_ref, raw, major, rows, ids, spots, spots_s, stage,
+                 table_sems, spot_sem, id_send, id_recv, far_send, far_recv, side_send, side_recv):
     feats, vocab = table_ref.shape
+    z = lax.axis_index("z"); xlo = lax.axis_index("xlo"); core = lax.axis_index("core")
+    xhi = lax.axis_index("xhi"); y = lax.axis_index("y")
+    me = ((z * 2 + xlo) * 2 + core) * 2 + xhi
+    groups = out_ref.shape[0]
+    up = (y + 1) % 4
+    down = (y + 3) % 4
     tiles = vocab // 128
-    count = sems.shape[0]
+    count = table_sems.shape[0]
     ends = [tiles * k // count for k in range(count + 1)]
     copies = []
     for k in range(count):
         part = pl.ds(ends[k] * 128, (ends[k + 1] - ends[k]) * 128)
-        copies.append(pltpu.make_async_copy(table_ref.at[:, part], raw.at[:, part], sems.at[k]))
+        copies.append(pltpu.make_async_copy(table_ref.at[:, part], raw.at[:, part], table_sems.at[k]))
     for copy in copies:
         copy.start()
+    barrier = pltpu.get_barrier_semaphore()
+    for k in range(1, 4):
+        pl.semaphore_signal(barrier, inc=1, device_id=place(me, (y + k) % 4), device_id_type=MESH)
+    def greet(k, _):
+        pl.semaphore_signal(barrier, inc=1, device_id=place((me + k) % groups, y), device_id_type=MESH)
+        return 0
+    lax.fori_loop(1, groups, greet, 0)
+    pl.semaphore_wait(barrier, 3 + groups - 1)
+    ids[pl.ds(me, 1), pl.ds(y, 1), :] = ids_ref[...][None]
+    line = []
+    for k in range(1, 4):
+        c = pltpu.make_async_remote_copy(ids_ref, ids.at[me, pl.ds(y, 1)], id_send.at[k - 1], id_recv.at[k - 1],
+            device_id=place(me, (y + k) % 4), device_id_type=MESH)
+        c.start(); line.append(c)
+
     for copy in copies:
         copy.wait()
 
@@ -44,59 +69,123 @@
         major[pl.ds(pl.multiple_of(b * 128, 128), 128), :] = block.T.astype(jnp.float32)
         return 0
 
-    lax.fori_loop(0, BLOCKS, turn, 0, unroll=12)
-    eye = (
-        lax.broadcasted_iota(jnp.int32, (128, 128), 0)
-        == lax.broadcasted_iota(jnp.int32, (128, 128), 1)
-    ).astype(jnp.bfloat16)
-    prompt = rows.shape[0]
-
-    def group(g, _):
+    half = BLOCKS // 4
+    lax.fori_loop(0, half, turn, 0, unroll=9)
+    for c in line:
+        c.wait()
+    def spread(k, _):
+        to = (me + k) % groups
+        pltpu.make_async_remote_copy(ids.at[me], ids.at[me], id_send.at[3], id_recv.at[3],
+            device_id=place(to, y), device_id_type=MESH).start()
+        return 0
+    lax.fori_loop(1, groups, spread, 0)
+    lax.fori_loop(half, BLOCKS, turn, 0, unroll=9)
+    others = pltpu.make_async_remote_copy(ids.at[pl.ds(0, groups - 1)], ids.at[pl.ds(0, groups - 1)], id_send.at[3], id_recv.at[3],
+        device_id=place(me, up), device_id_type=MESH)
+    others.wait_recv()
+    all_ids = ids[...]
+    strip_of = jnp.zeros_like(all_ids)
+    for k in range(1, 4):
+        strip_of = strip_of + jnp.where(all_ids >= k * STRIP, 1, 0)
+    spots[...] = all_ids - strip_of * STRIP
+    to_smem = pltpu.make_async_copy(spots, spots_s, spot_sem)
+    to_smem.start()
+    to_smem.wait()
+    eye = (lax.broadcasted_iota(jnp.int32, (128, 128), 0) == lax.broadcasted_iota(jnp.int32, (128, 128), 1)).astype(jnp.bfloat16)
+
+    def find(g, put):
         def some(s, _):
             for i in range(128):
-                rows[pl.ds(s * 128 + i, 1), :] = major[pl.ds(row_ref[g * prompt + s * 128 + i], 1), :]
+                rows[pl.ds(s * 128 + i, 1), :] = major[pl.ds(spots_s[g, s, i], 1), :]
             return 0
-
-        lax.fori_loop(0, prompt // 128, some, 0)
-        found = lax.dot_general(
-            eye,
-            rows[...].astype(jnp.bfloat16),
-            (((1,), (1,)), ((), ())),
-            preferred_element_type=jnp.float32,
-        )
-        strip = strip_ref[pl.ds(g, 1), :]
-        chosen = found[:feats]
-        for k in range(1, 4):
-            chosen = jnp.where(strip == k, found[k * feats : (k + 1) * feats], chosen)
-        out_ref[pl.ds(g, 1)] = chosen.astype(jnp.bfloat16)[None]
-        return 0
-
-    lax.fori_loop(0, out_ref.shape[0], group, 0)
-
-
-def lookup(table, ids, prompt):
+        lax.fori_loop(0, 4, some, 0)
+        found = lax.dot_general(eye, rows[...].astype(jnp.bfloat16), (((1,), (1,)), ((), ())), preferred_element_type=jnp.float32)
+        for s in range(4):
+            word = ids[pl.ds(g, 1), pl.ds(s, 1), :].reshape(1, 128)
+            part = found[:, s * 128:(s + 1) * 128]
+            chosen = part[:feats]
+            for k in range(1, 4):
+                chosen = jnp.where(word >= k * STRIP, part[k * feats:(k + 1) * feats], chosen)
+            put(s, chosen.astype(jnp.bfloat16))
+
+    def chunk(p, lo, n):
+        zs = (z + 4 - p) % 4
+        return pl.ds(zs * 8 + lo, n)
+
+    def side(p, way, lo, n, of, to, slot):
+        part = out_ref.at[chunk(p, lo, n), of]
+        return pltpu.make_async_remote_copy(part, part, side_send.at[slot, p], side_recv.at[slot, p],
+            device_id=place(me, to), device_id_type=MESH)
+
+    def relay(p):
+        side(p, 0, 0, 8, down, up, 0).wait_recv()
+        side(p, 0, 0, 4, down, up, 2).start()
+        side(p, 0, 0, 8, up, down, 1).wait_recv()
+        side(p, 0, 4, 4, up, down, 3).start()
+
+    for p in range(4):
+        if p == 0:
+            def put_own(s, val):
+                out_ref[pl.ds(me, 1), pl.ds(y, 1), :, s * 128:(s + 1) * 128] = val[None, None]
+            find(me, put_own)
+        def one(e, _):
+            to_z = (z + p) % 4
+            to = ((to_z * 2 + (xlo + e // 4) % 2) * 2 + (core + e // 2) % 2) * 2 + (xhi + e) % 2
+            def put(s, val):
+                stage[p, pl.ds(e, 1), :, s * 128:(s + 1) * 128] = val[None]
+            find(to, put)
+            pltpu.make_async_remote_copy(stage.at[p, e], out_ref.at[me, y], far_send.at[p], far_recv.at[p],
+                device_id=place(to, y), device_id_type=MESH).start()
+            return 0
+        lax.fori_loop(1 if p == 0 else 0, 8, one, 0)
+        n = 7 if p == 0 else 8
+        pltpu.make_async_remote_copy(stage.at[p, pl.ds(0, n)], out_ref.at[pl.ds(0, n), y], far_send.at[p], far_recv.at[p],
+            device_id=place(me, up), device_id_type=MESH).wait_recv()
+        side(p, 0, 0, 8, y, up, 0).start()
+        side(p, 0, 0, 8, y, down, 1).start()
+        if p:
+            relay(p - 1)
+    relay(3)
+    others.wait_send()
+    for p in range(4):
+        n = 7 if p == 0 else 8
+        pltpu.make_async_remote_copy(stage.at[p, pl.ds(0, n)], out_ref.at[pl.ds(0, n), y], far_send.at[p], far_recv.at[p],
+            device_id=place(me, up), device_id_type=MESH).wait_send()
+        side(p, 0, 0, 4, down, up, 2).wait_recv()
+        side(p, 0, 4, 4, up, down, 3).wait_recv()
+        side(p, 0, 0, 8, y, up, 0).wait_send()
+        side(p, 0, 0, 8, y, down, 1).wait_send()
+        side(p, 0, 0, 4, down, up, 2).wait_send()
+        side(p, 0, 4, 4, up, down, 3).wait_send()
+
+
+def front(table, ids):
     feats, vocab = table.shape
-    groups = ids.shape[0] // prompt
-    strip = ids // STRIP
-    row = ids - strip * STRIP
     return pl.pallas_call(
-        lookup_kernel,
-        out_shape=jax.ShapeDtypeStruct((groups, feats, prompt), jnp.bfloat16),
-        in_specs=[
-            pl.BlockSpec(memory_space=pltpu.SMEM),
-            pl.BlockSpec(memory_space=pltpu.VMEM),
-            pl.BlockSpec(memory_space=pl.ANY),
-        ],
+        front_kernel,
+        out_shape=jax.ShapeDtypeStruct((32, 4, feats, 512), jnp.bfloat16),
+        in_specs=[pl.BlockSpec(memory_space=pltpu.VMEM), pl.BlockSpec(memory_space=pl.ANY)],
         out_specs=pl.BlockSpec(memory_space=pltpu.VMEM),
         scratch_shapes=[
             pltpu.VMEM((feats, vocab), jnp.bfloat16),
             pltpu.VMEM((STRIP, 128), jnp.float32),
-            pltpu.VMEM((prompt, 128), jnp.float32),
+            pltpu.VMEM((512, 128), jnp.float32),
+            pltpu.VMEM((32, 4, 128), jnp.int32),
+            pltpu.VMEM((32, 4, 128), jnp.int32),
+            pltpu.SMEM((32, 4, 128), jnp.int32),
+            pltpu.VMEM((4, 8, feats, 512), jnp.bfloat16),
             pltpu.SemaphoreType.DMA((6,)),
+            pltpu.SemaphoreType.DMA,
+            pltpu.SemaphoreType.DMA((4,)),
+            pltpu.SemaphoreType.DMA((4,)),
+            pltpu.SemaphoreType.DMA((4,)),
+            pltpu.SemaphoreType.DMA((4,)),
+            pltpu.SemaphoreType.DMA((4, 4)),
+            pltpu.SemaphoreType.DMA((4, 4)),
         ],
-        compiler_params=pltpu.CompilerParams(vmem_limit_bytes=50 * 2**20),
-        cost_estimate=pl.CostEstimate(flops=30_000_000_000, bytes_accessed=8_000_000, transcendentals=0),
-    )(row, strip.reshape(groups, prompt), table)
+        compiler_params=pltpu.CompilerParams(vmem_limit_bytes=50 * 2**20, collective_id=0, has_side_effects=True),
+        cost_estimate=pl.CostEstimate(flops=60_000_000_000, bytes_accessed=8_000_000, transcendentals=0),
+    )(ids.reshape(1, 128), table)
 
 
 def rotate(heads_in, positions):
@@ -140,8 +229,6 @@
     member = lax.axis_index("y")
     group_index = lax.axis_index(("z", "xlo", "core", "xhi"))
     length = lax.dynamic_slice_in_dim(prompt_lengths, group_index, 1, 0)[0]
-    all_ids = lax.all_gather(prompt_ids, AXES, axis=0, tiled=True)
-
     query_width = w_query.shape[1]
     key_width = w_key.shape[1]
     packed = jnp.concatenate([w_query, w_key, w_value], axis=1)
@@ -149,13 +236,7 @@
     wide = wide.reshape(2, model_width, packed.shape[1])
     out_parts = lax.all_gather(w_out, ("xhi", "z", "xlo", "core"), axis=0, tiled=False)
 
-    picked = lookup(embed_table, all_ids, row_count)
-    group_count = devices // TPG
-    outgoing = jnp.broadcast_to(
-        picked[:, None], (group_count, TPG, features, row_count)
-    ).reshape(devices, features, row_count)
-    arrived = lax.all_to_all(outgoing, AXES, split_axis=0, concat_axis=0, tiled=True)
-    tokens = arrived.reshape(model_width, row_count)
+    tokens = front(embed_table, prompt_ids).reshape(model_width, row_count)
     wide_in = tokens.astype(jnp.float32)
     scale = lax.rsqrt(jnp.mean(wide_in * wide_in, axis=0, keepdims=True) + norm_eps)
     normed = (wide_in * scale * norm_gain[:, None]).astype(jnp.bfloat16)

time: 556 us -> 281 us (0.51)
  blocking collectives: 319 us -> 0 us
  Pallas kernels: 28.1 us -> 72.3 us
  local copies, waits for them, and re-layouts: 16.1 us -> 28.8 us
  waiting for transfers between devices: 114 us -> 103 us
    all_gather x1 -> x0, blocking collectives: 319 us -> none  [shards(): all_ids = lax.all_gather(prompt_ids, AXES, axis=0, tiled=True)]
    all_to_all x1 -> x0, waiting for transfers between devices: 47.7 us -> none  [shards(): lax.all_to_all(outgoing, AXES, split_axis=0, concat_axis=0, tiled=True)]
    pallas_call x1, Pallas kernels: 28.1 us -> 72.3 us  [front(): pl.pallas_call(front_kernel, out_shape=jax.ShapeDtypeStruct((32, 4, feats...]
    all_gather x1, waiting for transfers between devices: 0.02 us -> 38.8 us  [shards(): lax.all_gather(w_out, ('xhi', 'z', 'xlo', 'core'), axis=0, tiled=False)]
    ppermute x2, waiting for transfers between devices: 65.9 us -> 51.6 us  [swapped(): return lax.ppermute(block, 'y', [(k, k ^ 1 << apart) for k in range(TPG)])]
    all_gather x1, waiting for transfers between devices: 0.01 us -> 11.6 us  [shards(): lax.all_gather(packed, ('xhi', 'z', 'xlo', 'core'), axis=0, tiled=True)]
    convert_element_type x0 -> x2, local copies, waits for them, and re-layouts: none -> 9.7 us  [the longest x1 5.61 us: shards(): running = kept.astype(jnp.float32) + arrived_sum.astype(jnp.float32)]
    all_to_all x1 -> x0, starting transfers between devices: 5.97 us -> none  [shards(): lax.all_to_all(outgoing, AXES, split_axis=0, concat_axis=0, tiled=True)]
  transfers between devices with their start and end apart: 5 -> 4, of which waited for: 3 -> 4; matrix products, arithmetic and copies ran while one was open for 8% -> 21% of each run, Pallas kernels for 5% -> 26%
where the time goes in v2:
time: 281 us; the launch traced here: 280 us
  waiting for transfers between devices  103 us (37%)
  Pallas kernels  72.3 us (26%)
  other arithmetic  30.9 us (11%)
  local copies, waits for them, and re-layouts  28.8 us (10%)
  matrix products  26.9 us (10%)
  between operations  14.2 us (5%)
  starting transfers between devices  4.5 us (2%)
    pallas_call x1, Pallas kernels, front(): pl.pallas_call(front_kernel, out_shape=jax.ShapeDtypeStruct((32, 4, feats...  72.3 us
    ppermute x2, waiting for transfers between devices, swapped(): return lax.ppermute(block, 'y', [(k, k ^ 1 << apart) for k in range(TPG)])  51.6 us
    all_gather x1, waiting for transfers between devices, shards(): lax.all_gather(w_out, ('xhi', 'z', 'xlo', 'core'), axis=0, tiled=False)  38.8 us
    all_gather x1, waiting for transfers between devices, shards(): lax.all_gather(packed, ('xhi', 'z', 'xlo', 'core'), axis=0, tiled=True)  11.6 us
    dot_general x1, matrix products, shards(): jnp.einsum('dr,kdc->rkc', normed, wide, preferred_element_type=jnp.float32)  10.7 us
    dot_general x1, matrix products, shards(): jnp.einsum('rkw,kdwc->rdc', attended, out_wide, preferred_element_type=jn...  10.3 us
    unnamed x12, local copies, waits for them, and re-layouts  5.73 us
    sub x1, other arithmetic, attend(): expd = jnp.exp(scores - biggest)  5.69 us
  transfers between devices with their start and end apart: 4, of which 4 were waited for; matrix products, arithmetic and copies ran while one was open for 21% of the time, Pallas kernels for 26%

profile of v2, /device:TPU:0, one launch (start us, length us, event | category | flops | bytes accessed | tf_op | source)
XLA Modules:
  0.0 280.3 jit_solution(3081636046605125858)
XLA Ops:
  7.2 1.8 pad_maximum_fusion
  12.9 1.3 dynamic_slice.7
  15.5 72.3 %shard_map.95 = bf16[32,4,32,512]{3,2,1,0:T(8,128)(2,1)} custom-call(s32[1,128]{1,0:T(1,128)S(1)} %bitcast.60, bf16[32,128256]{1,0:T(8,128)(2,1)} %table_ref.1), custom_call_target="tpu_custom_call" | custom-call | flops 60000002048 | bytes 8000000 | tf_op jit(solution)/shard_map/pallas_call | solution.py:164
  87.8 3.4 %fusion.1 = f32[512]{0:T(512)S(1)} fusion(bf16[32,4,32,512]{3,2,1,0:T(8,128)(2,1)} %shard_map.95), kind=kLoop, calls=%fused_computation.3 | loop fusion | flops 6290944 | bytes 4196352 | tf_op jit(solution)/shard_map/reduce_sum | solution.py:241
  92.1 2.5 fusion.3
  94.7 11.6 %all-gather.4.cloned.1.call-done = bf16[8192,768]{1,0:T(8,128)(2,1)} async-done(((bf16[256,768]{1,0:T(8,128)(2,1)}), bf16[8192,768]{1,0:T(8,128)(2,1)}) %all-gather.4.cloned.1.call-update) | async-done | bytes 12582928 | tf_op jit(solution)/shard_map/all_gather | solution.py:235
  106.2 10.7 %fusion.23 = f32[512,2,768]{2,0,1:T(8,128)S(1)} fusion(bf16[4096,512,1]{1,0,2:T(8,128)(2,1)} %bitcast.64, bf16[2,4096,768]{2,1,0:T(8,128)(2,1)} %bitcast.69), kind=kOutput, calls=%fused_computation.52 | convolution fusion | flops 6442450944 | bytes 19922944 | tf_op jit(solution)/shard_map/dr,kdc->rkc/dot_general | solution.py:245
  116.9 1.7 copy-done.3
  118.6 1.7 slice.53
  120.3 1.9 copy.37
  123.6 1.7 multiply_subtract_fusion
  125.4 1.3 fusion.11
  126.7 5.7 %fusion.21 = (f32[2,4,512]{2,1,0:T(4,128)S(1)}, f32[2,4,512,512]{2,3,1,0:T(8,128)}) fusion(f32[2,512,512,4]{2,1,3,0:T(8,128)S(1)} %fusion.11, pred[512,512]{0,1:T(8,128)(4,1)S(1)} %copy-done.4), kind=kOutput, calls=%fused_computation.50 | output fusion | flops 12583423 | bytes 17055744 | tf_op jit(solution)/shard_map/sub | solution.py:213
  132.4 4.5 %fusion.10 = bf16[2,128,4,512]{3,1,2,0:T(8,128)(2,1)S(1)} fusion(f32[2,4,512,512]{2,3,1,0:T(8,128)} %get-tuple-element.15, f32[2,4,512]{2,1,0:T(4,128)S(1)} %get-tuple-element.14, f32[512,2,768]{2,0,1:T(8,128)} %copy-done.3), kind=kOutput, calls=%fused_computation.23 | convolution fusion | flops 541589504 | bytes 9715712 | tf_op jit(solution)/shard_map/hgqk,khd->qhgd/dot_general | solution.py:215
  137.0 38.8 %all-gather.6.cloned.1.call-done = bf16[16384,256]{1,0:T(8,128)(2,1)} async-done(((bf16[512,256]{1,0:T(8,128)(2,1)}), bf16[16384,256]{1,0:T(8,128)(2,1)}) %all-gather.6.cloned.1.call-update) | async-done | bytes 8388624 | tf_op jit(solution)/shard_map/all_gather | solution.py:237
  175.8 10.3 %convolution_bitcast_fusion = bf16[512,16,256]{0,2,1:T(8,128)(2,1)S(1)} fusion(bf16[512,2,512,1]{0,2,3,1:T(8,128)(2,1)S(1)} %bitcast.71, bf16[2,16,512,256]{3,2,1,0:T(8,128)(2,1)} %bitcast.70), kind=kOutput, calls=%fused_computation.17 | convolution fusion | flops 4294967296 | bytes 13631488 | tf_op jit(solution)/shard_map/rkw,kdwc->rdc/dot_general | solution.py:264
  186.1 1.6 select_convert_fusion
  187.7 4.1 %copy.44 = bf16[256,4096]{1,0:T(8,128)(2,1)} copy(bf16[256,4096]{0,1:T(8,128)(2,1)} %bitcast.63) | data formatting | bytes 4194304 | tf_op jit(solution)/shard_map/convert_element_type | solution.py:272
  191.7 3.0 %collective-permute-start = (bf16[256,4096]{1,0:T(8,128)(2,1)}, bf16[256,4096]{1,0:T(8,128)(2,1)}, u32[]{:S(2)}, u32[]{:S(2)}) collective-permute-start(bf16[256,4096]{1,0:T(8,128)(2,1)} %copy.44), channel_id=1, source_target_pairs={{0,2},{1,3},{2,0},{3,1},{4,6},{5,7},{6,4},{7,5},{8,10},{9,11},{10,... | collective-permute-start | bytes 6291464 | tf_op jit(solution)/shard_map/ppermute | solution.py:220
  194.7 2.4 bitcast_convert_fusion
  197.2 5.6 %copy.45 = f32[256,4096]{1,0:T(8,128)} copy(f32[256,4096]{0,1:T(8,128)} %bitcast_convert_fusion) | data formatting | bytes 8388608 | tf_op jit(solution)/shard_map/convert_element_type | solution.py:274
  202.8 38.5 %collective-permute-done = bf16[256,4096]{1,0:T(8,128)(2,1)} collective-permute-done((bf16[256,4096]{1,0:T(8,128)(2,1)}, bf16[256,4096]{1,0:T(8,128)(2,1)}, u32[]{:S(2)}, u32[]{:S(2)}) %collective-permute-start) | collective-permute-done | bytes 2097184 | tf_op jit(solution)/shard_map/ppermute | solution.py:220
  241.3 3.4 %convert_add_fusion = bf16[256,4096]{1,0:T(8,128)(2,1)S(1)} fusion(f32[256,4096]{1,0:T(8,128)} %copy.45, bf16[256,4096]{1,0:T(8,128)(2,1)} %collective-permute-done), kind=kLoop, calls=%fused_computation.10 | loop fusion | flops 3145728 | bytes 8388608 | tf_op jit(solution)/shard_map/add | solution.py:274
  245.8 1.4 collective-permute-start.1
  247.3 1.3 constant_dynamic-slice_fusion
  248.6 1.3 copy.61
  249.9 1.9 slice.81
  252.6 1.1 copy.47
  253.7 1.8 maximum_bitcast_fusion
  255.5 2.0 copy.48
  257.5 13.0 %collective-permute-done.1 = bf16[128,4096]{1,0:T(8,128)(2,1)} collective-permute-done((bf16[128,4096]{1,0:T(8,128)(2,1)}, bf16[128,4096]{1,0:T(8,128)(2,1)}, u32[]{:S(2)}, u32[]{:S(2)}) %collective-permute-start.1) | collective-permute-done | bytes 1048608 | tf_op jit(solution)/shard_map/ppermute | solution.py:220
  270.6 2.8 %fusion.9 = bf16[128,4096]{1,0:T(8,128)(2,1)} fusion(bf16[4096,128]{0,1:T(8,128)(2,1)S(1)} %copy-done.2, bf16[128,4096]{1,0:T(8,128)(2,1)} %collective-permute-done.1, bf16[256,4096]{1,0:T(8,128)(2,1)S(1)} %convert_add_fusion, pred[]{:T(512)S(6)} %eq.6), kind=kLoop, calls=%fused_computation.20 | loop fusion | flops 3670016 | bytes 5242881 | tf_op jit(solution)/shard_map/convert_element_type | solution.py:275
  (28 shorter events, 9.4 us)
Async XLA Ops:
  7.2 99.1 %all-gather.4.cloned.1.call-start = ((), (), s32[]{:S(2)}) async-start(), calls=%async_computation | async-start | bytes 12976128 | tf_op jit(solution)/shard_map/all_gather | solution.py:235
  9.0 166.7 %all-gather.6.cloned.1.call-start = ((), (), s32[]{:S(2)}) async-start(), calls=%async_computation.1 | async-start | bytes 8650752 | tf_op jit(solution)/shard_map/all_gather | solution.py:237
  14.8 0.7 copy-start
  87.8 4.3 %copy-start.1 = (bf16[32,4,32,512]{3,2,1,0:T(8,128)(2,1)S(1)}, bf16[32,4,32,512]{3,2,1,0:T(8,128)(2,1)}, u32[]{:S(2)}) copy-start(bf16[32,4,32,512]{3,2,1,0:T(8,128)(2,1)} %shard_map.95) | copy-start | bytes 12582916
  116.9 1.7 copy-start.3
  125.4 1.4 copy-start.4
  191.7 49.6 %collective-permute-start = (bf16[256,4096]{1,0:T(8,128)(2,1)}, bf16[256,4096]{1,0:T(8,128)(2,1)}, u32[]{:S(2)}, u32[]{:S(2)}) collective-permute-start(bf16[256,4096]{1,0:T(8,128)(2,1)} %copy.44), channel_id=1, source_target_pairs={{0,2},{1,3},{2,0},{3,1},{4,6},{5,7},{6,4},{7,5},{8,10},{9,11},{10,... | collective-permute-start | bytes 6291464 | tf_op jit(solution)/shard_map/ppermute | solution.py:220
  245.8 24.7 %collective-permute-start.1 = (bf16[128,4096]{1,0:T(8,128)(2,1)}, bf16[128,4096]{1,0:T(8,128)(2,1)}, u32[]{:S(2)}, u32[]{:S(2)}) collective-permute-start(bf16[128,4096]{1,0:T(8,128)(2,1)} %select_convert_fusion.2), channel_id=1, source_target_pairs={{0,1},{1,0},{2,3},{3,2},{4,5},{5,4},{6,7},{7,6},{8,9},{9,8},{10,11... | collective-permute-start | bytes 3145736 | tf_op jit(solution)/shard_map/ppermute | solution.py:220
  249.9 20.7 %copy-start.2 = (bf16[4096,128]{0,1:T(8,128)(2,1)S(1)}, bf16[4096,128]{0,1:T(8,128)(2,1)}, u32[]{:S(2)}) copy-start(bf16[4096,128]{0,1:T(8,128)(2,1)} %copy.61) | copy-start | bytes 3145732
Sparse Core Ops, SparseCore 0:
  10.3 95.9 all-gather.3
  107.9 67.7 all-gather.5

commit v3 on v2

--- a/solution.py
+++ b/solution.py
@@ -1,13 +1,12 @@
 import jax
 import jax.numpy as jnp
+import numpy as np
 from jax import lax
 from jax.experimental import pallas as pl
 from jax.experimental.pallas import tpu as pltpu
 from jax.sharding import Mesh
 from jax.sharding import PartitionSpec as P
 
-HEADS = 32
-KVH = 8
 HD = 128
 TPG = 4
 AXES = ("z", "xlo", "core", "xhi", "y")
@@ -188,92 +187,222 @@
     )(ids.reshape(1, 128), table)
 
 
-def rotate(heads_in, positions):
-    half = heads_in.shape[-1] // 2
-    freq = rope_theta ** (-2.0 * jnp.arange(half, dtype=jnp.float32) / heads_in.shape[-1])
-    angle = positions.astype(jnp.float32)[:, None] * freq[None, :]
-    cosine = jnp.cos(angle)[:, None, :]
-    sine = jnp.sin(angle)[:, None, :]
-    first = heads_in[..., :half]
-    second = heads_in[..., half:]
-    return jnp.concatenate(
-        [first * cosine - second * sine, second * cosine + first * sine], axis=-1
-    )
-
-
-def attend(query_rot, key_rot, value_rows, length):
-    row_count = query_rot.shape[0]
-    positions = jnp.arange(row_count, dtype=jnp.int32)
-    scores = jnp.einsum(
-        "qhgd,khd->hgqk", query_rot, key_rot, preferred_element_type=jnp.float32
-    ) / jnp.sqrt(jnp.float32(HD))
-    allowed = (positions[None, :] <= positions[:, None]) & (positions[None, :] < length)
-    scores = jnp.where(allowed, scores, -1e30)
-    biggest = jnp.max(scores, axis=-1, keepdims=True)
-    expd = jnp.exp(scores - biggest)
-    weights = (expd / jnp.sum(expd, axis=-1, keepdims=True)).astype(jnp.bfloat16)
-    result = jnp.einsum("hgqk,khd->qhgd", weights, value_rows, preferred_element_type=jnp.float32)
-    return result.astype(jnp.bfloat16).reshape(row_count, -1)
-
-
-def swapped(block, apart):
-    return lax.ppermute(block, "y", [(k, k ^ 1 << apart) for k in range(TPG)])
+def back_kernel(lens_ref, tokens_ref, gain_ref, cos_ref, sin_ref, w_ref, wo_ref, hidden_ref, cache_ref,
+                turned, w, wo, x, normed, squares, q, k, v, attended, stage, mid, passed, final,
+                load_sems, far_send, far_recv, near_send, near_recv, sum_send, sum_recv):
+    z = lax.axis_index("z"); xlo = lax.axis_index("xlo"); core = lax.axis_index("core")
+    xhi = lax.axis_index("xhi"); y = lax.axis_index("y")
+    me = ((z * 2 + xlo) * 2 + core) * 2 + xhi
+    width, prompt = turned.shape
+    quarter = prompt // 4
+    up = (y + 1) % 4
+    down = (y + 3) % 4
+    far = (y + 2) % 4
+
+    def at(member):
+        return (z, xlo, core, xhi, member)
+
+    loads = [
+        pltpu.make_async_copy(tokens_ref, turned, load_sems.at[0]),
+        pltpu.make_async_copy(w_ref, w, load_sems.at[1]),
+        pltpu.make_async_copy(wo_ref, wo, load_sems.at[2]),
+    ]
+    for load in loads:
+        load.start()
+    barrier = pltpu.get_barrier_semaphore()
+    for member in (up, down):
+        pl.semaphore_signal(barrier, inc=1, device_id=at(member), device_id_type=MESH)
+    pl.semaphore_wait(barrier, 2)
+
+    loads[0].wait()
+    squares[...] = jnp.zeros_like(squares)
+
+    def turn(c, _):
+        cols = pl.ds(pl.multiple_of(c * 128, 128), 128)
+        piece = turned[cols, :].T
+        x[:, cols] = piece
+        wide = piece.astype(jnp.float32)
+        squares[...] += wide * wide
+        return 0
+
+    lax.fori_loop(0, width // 128, turn, 0, unroll=2)
+    scale = lax.rsqrt(jnp.sum(squares[...], axis=1, keepdims=True) / width + norm_eps)
+    squares[...] = jnp.broadcast_to(scale, squares.shape)
+
+    def norm(c, _):
+        cols = pl.ds(pl.multiple_of(c * 128, 128), 128)
+        wide = x[:, cols].astype(jnp.float32) * squares[...] * gain_ref[:, cols]
+        normed[:, cols] = wide.astype(jnp.bfloat16)
+        return 0
+
+    lax.fori_loop(0, width // 128, norm, 0, unroll=2)
+    loads[1].wait()
+
+    def rotated(part):
+        return (part * cos_ref[...] + pltpu.roll(part, HD // 2, 1) * sin_ref[...]).astype(jnp.bfloat16)
+
+    def query(i, _):
+        b = i // 2
+        cols = pl.ds(pl.multiple_of(i % 2 * 256, 256), 256)
+        both = jnp.dot(normed[...], w[b, :, cols], preferred_element_type=jnp.float32)
+        for h in range(2):
+            q[pl.ds(i * 2 + h, 1)] = rotated(both[:, h * HD : (h + 1) * HD])[None]
+        return 0
+
+    lax.fori_loop(0, 4, query, 0)
+
+    for b in range(2):
+        both = jnp.dot(normed[...], w[b, :, 512:768], preferred_element_type=jnp.float32)
+        key = rotated(both[:, :HD])
+        value = both[:, HD:].astype(jnp.bfloat16)
+        k[b] = key
+        v[b] = value
+        cache_ref[0, 0, :, b * HD : (b + 1) * HD] = key
+        cache_ref[0, 1, :, b * HD : (b + 1) * HD] = value
+
+    length = lens_ref[me]
+
+    def head(h, _):
+        b = h // 4
+        for r in range(4):
+            rows = slice(r * quarter, (r + 1) * quarter)
+            keys = (r + 1) * quarter
+            scores = lax.dot_general(q[h, rows, :], k[b, :keys, :], (((1,), (1,)), ((), ())), preferred_element_type=jnp.float32)
+            scores = scores * np.float32(1 / np.sqrt(HD))
+            p = lax.broadcasted_iota(jnp.int32, (quarter, keys), 0) + r * quarter
+            j = lax.broadcasted_iota(jnp.int32, (quarter, keys), 1)
+            scores = jnp.where((j <= p) & (j < length), scores, -1e30)
+            expd = jnp.exp(scores - jnp.max(scores, axis=1, keepdims=True))
+            weights = (expd / jnp.sum(expd, axis=1, keepdims=True)).astype(jnp.bfloat16)
+            got = jnp.dot(weights, v[b, :keys, :], preferred_element_type=jnp.float32)
+            attended[rows, pl.ds(pl.multiple_of(h * HD, HD), HD)] = got.astype(jnp.bfloat16)
+        return 0
+
+    lax.fori_loop(0, 8, head, 0)
+    loads[2].wait()
+
+    def send(src, dst, ssem, rsem, member):
+        return pltpu.make_async_remote_copy(src, dst, ssem, rsem, device_id=at(member), device_id_type=MESH)
+
+    def far_copy(c, way):
+        return send(stage.at[c, far, way], mid.at[c, way], far_send.at[c, way], far_recv.at[c, way], down if way else up)
+
+    def near_copy(c, way):
+        return send(stage.at[c, down if way else up, 1 - way], final.at[c, way, 1 - way], near_send.at[c, way], near_recv.at[c, way], down if way else up)
+
+    def sum_copy(c, way):
+        return send(passed.at[c, way], final.at[c, way, way], sum_send.at[c, way], sum_recv.at[c, way], down if way else up)
+
+    def pass_on(c):
+        for way in range(2):
+            far_copy(c, way).wait_recv()
+            mine = stage[pl.ds(c, 1), pl.ds(down if way else up, 1), way].reshape(quarter, 256)
+            passed[pl.ds(c, 1), way] = (mine.astype(jnp.float32) + mid[pl.ds(c, 1), way].reshape(quarter, 256).astype(jnp.float32)).astype(jnp.bfloat16)[None]
+            sum_copy(c, way).start()
+
+    def finish(c):
+        for way in range(2):
+            near_copy(c, way).wait_recv()
+            sum_copy(c, way).wait_recv()
+        own = pl.ds(pl.multiple_of(y * quarter, quarter), quarter)
+        for half in range(2):
+            cols = pl.ds(pl.multiple_of(c * 512 + half * 256, 256), 256)
+            total = stage[pl.ds(c, 1), pl.ds(y, 1), half].reshape(quarter, 256).astype(jnp.float32)
+            for way in range(2):
+                total = total + final[pl.ds(c, 1), way, half].reshape(quarter, 256).astype(jnp.float32)
+            hidden_ref[:, cols] = (x[own, cols].astype(jnp.float32) + total).astype(jnp.bfloat16)
+
+    chunks = stage.shape[0]
+
+    def project(c, _):
+        for half in range(2):
+            part = jnp.dot(attended[:, :512], wo[0, c * 2 + half], preferred_element_type=jnp.float32)
+            part = part + jnp.dot(attended[:, 512:], wo[1, c * 2 + half], preferred_element_type=jnp.float32)
+            part = part.astype(jnp.bfloat16)
+            for member in range(4):
+                stage[pl.ds(c, 1), member, half] = part[member * quarter : (member + 1) * quarter][None]
+        for way in range(2):
+            far_copy(c, way).start()
+        for way in range(2):
+            near_copy(c, way).start()
+
+        @pl.when(c > 0)
+        def _():
+            pass_on(c - 1)
+
+        return 0
+
+    lax.fori_loop(0, chunks, project, 0)
+    pass_on(chunks - 1)
+
+    def last(c, _):
+        finish(c)
+        return 0
+
+    lax.fori_loop(0, chunks, last, 0)
+
+    def drain(c, _):
+        for way in range(2):
+            far_copy(c, way).wait_send()
+            near_copy(c, way).wait_send()
+            sum_copy(c, way).wait_send()
+        return 0
+
+    lax.fori_loop(0, chunks, drain, 0)
+
+
+def back(lengths, tokens, gain, w, wo):
+    width, prompt = tokens.shape
+    quarter = prompt // 4
+    angle = np.arange(prompt)[:, None] * rope_theta ** (-2.0 * np.arange(HD // 2) / HD)[None, :]
+    cosine = np.concatenate([np.cos(angle), np.cos(angle)], axis=1).astype(np.float32)
+    sine = np.concatenate([-np.sin(angle), np.sin(angle)], axis=1).astype(np.float32)
+    chunks = width // 512
+    bf = jnp.bfloat16
+    vmem = pl.BlockSpec(memory_space=pltpu.VMEM)
+    anyw = pl.BlockSpec(memory_space=pl.ANY)
+    dma = pltpu.SemaphoreType.DMA
+    return pl.pallas_call(
+        back_kernel,
+        out_shape=(
+            jax.ShapeDtypeStruct((quarter, width), bf),
+            jax.ShapeDtypeStruct((1, 2, prompt, 2 * HD), bf),
+        ),
+        in_specs=[pl.BlockSpec(memory_space=pltpu.SMEM), anyw, vmem, vmem, vmem, anyw, anyw],
+        out_specs=(vmem, vmem),
+        scratch_shapes=[
+            pltpu.VMEM((width, prompt), bf),
+            pltpu.VMEM(w.shape, bf),
+            pltpu.VMEM(wo.shape, bf),
+            pltpu.VMEM((prompt, width), bf),
+            pltpu.VMEM((prompt, width), bf),
+            pltpu.VMEM((prompt, 128), jnp.float32),
+            pltpu.VMEM((8, prompt, HD), bf),
+            pltpu.VMEM((2, prompt, HD), bf),
+            pltpu.VMEM((2, prompt, HD), bf),
+            pltpu.VMEM((prompt, 1024), bf),
+            pltpu.VMEM((chunks, 4, 2, quarter, 256), bf),
+            pltpu.VMEM((chunks, 2, quarter, 256), bf),
+            pltpu.VMEM((chunks, 2, quarter, 256), bf),
+            pltpu.VMEM((chunks, 2, 2, quarter, 256), bf),
+            dma((3,)),
+        ] + [dma((chunks, 2))] * 6,
+        compiler_params=pltpu.CompilerParams(vmem_limit_bytes=58 * 2**20, collective_id=1, has_side_effects=True),
+        cost_estimate=pl.CostEstimate(flops=60_000_000_000, bytes_accessed=30_000_000, transcendentals=0),
+    )(lengths, tokens, gain.reshape(1, width), cosine, sine, w, wo)
 
 
 def shards(prompt_ids, prompt_lengths, embed_table, norm_gain, w_query, w_key, w_value, w_out):
-    quarter = prompt_ids.shape[0]
-    row_count = quarter * TPG
-    devices = lax.axis_size(AXES)
-    features = embed_table.shape[0]
-    model_width = features * devices
-    member = lax.axis_index("y")
-    group_index = lax.axis_index(("z", "xlo", "core", "xhi"))
-    length = lax.dynamic_slice_in_dim(prompt_lengths, group_index, 1, 0)[0]
-    query_width = w_query.shape[1]
-    key_width = w_key.shape[1]
+    row_count = prompt_ids.shape[0] * TPG
+    model_width = embed_table.shape[0] * lax.axis_size(AXES)
     packed = jnp.concatenate([w_query, w_key, w_value], axis=1)
-    wide = lax.all_gather(packed, ("xhi", "z", "xlo", "core"), axis=0, tiled=True)
+    plane = ("xhi", "z", "xlo", "core")
+    wide = lax.all_gather(packed, plane, axis=0, tiled=True)
     wide = wide.reshape(2, model_width, packed.shape[1])
-    out_parts = lax.all_gather(w_out, ("xhi", "z", "xlo", "core"), axis=0, tiled=False)
-
+    out_wide = lax.all_gather(w_out, plane, axis=0, tiled=False)
+    out_wide = out_wide.reshape(2, -1, *w_out.shape)
     tokens = front(embed_table, prompt_ids).reshape(model_width, row_count)
-    wide_in = tokens.astype(jnp.float32)
-    scale = lax.rsqrt(jnp.mean(wide_in * wide_in, axis=0, keepdims=True) + norm_eps)
-    normed = (wide_in * scale * norm_gain[:, None]).astype(jnp.bfloat16)
-    own_rows = lax.dynamic_slice_in_dim(tokens, member * quarter, quarter, 1).T
-
-    projected = jnp.einsum("dr,kdc->rkc", normed, wide, preferred_element_type=jnp.float32)
-    blocks = projected.shape[1]
-    local_heads = blocks * query_width // HD
-    local_kv = blocks * key_width // HD
-    positions = jnp.arange(row_count, dtype=jnp.int32)
-    query = projected[:, :, :query_width].reshape(row_count, local_heads, HD)
-    key_raw = projected[:, :, query_width : query_width + key_width]
-    value_rows = projected[:, :, query_width + key_width :].astype(jnp.bfloat16)
-    query_rot = rotate(query, positions).astype(jnp.bfloat16)
-    key_rot = rotate(key_raw, positions).astype(jnp.bfloat16)
-    cache = jnp.stack(
-        [key_rot.reshape(row_count, local_kv * HD), value_rows.reshape(row_count, local_kv * HD)],
-        axis=0,
-    )[None]
-    attended = attend(
-        query_rot.reshape(row_count, local_kv, HEADS // KVH, HD), key_rot, value_rows, length
-    )
-    attended = attended.reshape(row_count, blocks, query_width)
-    out_wide = out_parts.reshape(blocks, -1, query_width, out_parts.shape[-1])
-    partial_sum = jnp.einsum(
-        "rkw,kdwc->rdc", attended, out_wide, preferred_element_type=jnp.float32
-    ).reshape(row_count, model_width)
-    running = partial_sum
-    for bit_index in reversed(range(2)):
-        half_rows = running.shape[0] // 2
-        upper_half = member >> bit_index & 1 == 1
-        kept = jnp.where(upper_half, running[half_rows:], running[:half_rows]).astype(jnp.bfloat16)
-        given = jnp.where(upper_half, running[:half_rows], running[half_rows:]).astype(jnp.bfloat16)
-        arrived_sum = swapped(given, bit_index)
-        running = kept.astype(jnp.float32) + arrived_sum.astype(jnp.float32)
-    hidden = (own_rows.astype(jnp.float32) + running).astype(jnp.bfloat16)
-    return (hidden, cache)
+    return back(prompt_lengths, tokens, norm_gain, wide, out_wide)
 
 
 def solution(mesh):

time: 281 us -> 252 us (0.90)
  Pallas kernels: 72.3 us -> 140 us
  other arithmetic: 30.9 us -> 1.81 us
  matrix products: 26.9 us -> 0 us
  local copies, waits for them, and re-layouts: 28.8 us -> 4.81 us
  waiting for transfers between devices: 103 us -> 90.5 us
  starting transfers between devices: 4.5 us -> 0.08 us
    pallas_call x0 -> x1, Pallas kernels: none -> 68 us  [back(): pl.pallas_call(back_kernel, out_shape=(jax.ShapeDtypeStruct((quarter, wid...]
    ppermute x2 -> x0, waiting for transfers between devices: 51.6 us -> none  [swapped(): return lax.ppermute(block, 'y', [(k, k ^ 1 << apart) for k in range(TPG)])]
    all_gather x2, waiting for transfers between devices: 50.3 us -> 89.8 us  [the longest x1 78.6 us: shards(): wide = lax.all_gather(packed, plane, axis=0, tiled=True)]
    dot_general x4 -> x0, matrix products: 26.9 us -> none  [the longest x1 10.7 us: shards(): jnp.einsum('dr,kdc->rkc', normed, wide, preferred_element_type=jnp.float32)]
    convert_element_type x7 -> x0, other arithmetic: 10.6 us -> none  [the longest x1 2.84 us: shards(): hidden = (own_rows.astype(jnp.float32) + running).astype(jnp.bfloat16)]
    convert_element_type x3 -> x0, local copies, waits for them, and re-layouts: 10.6 us -> none  [the longest x1 5.61 us: shards(): running = kept.astype(jnp.float32) + arrived_sum.astype(jnp.float32)]
    sub x2 -> x0, other arithmetic: 7.34 us -> none  [the longest x1 5.69 us: attend(): expd = jnp.exp(scores - biggest)]
    slice x4 -> x0, local copies, waits for them, and re-layouts: 6.53 us -> none  [the longest x2 3.58 us: shards(): query = projected[:, :, :query_width].reshape(row_count, local_heads, HD)]
  transfers between devices with their start and end apart: 4 -> 2, of which waited for: 4 -> 2; matrix products, arithmetic and copies ran while one was open for 21% -> 1% of each run, Pallas kernels for 26% -> 29%
where the time goes in v3:
time: 252 us; the launch traced here: 251 us
  Pallas kernels  140 us (56%)
  waiting for transfers between devices  90.5 us (36%)
  between operations  14.1 us (6%)
  local copies, waits for them, and re-layouts  4.81 us (2%)
    all_gather x1, waiting for transfers between devices, shards(): wide = lax.all_gather(packed, plane, axis=0, tiled=True)  78.6 us
    pallas_call x1, Pallas kernels, front(): pl.pallas_call(front_kernel, out_shape=jax.ShapeDtypeStruct((32, 4, feats...  71.9 us
    pallas_call x1, Pallas kernels, back(): pl.pallas_call(back_kernel, out_shape=(jax.ShapeDtypeStruct((quarter, wid...  68 us
    all_gather x1, waiting for transfers between devices, shards(): out_wide = lax.all_gather(w_out, plane, axis=0, tiled=False)  11.2 us
  transfers between devices with their start and end apart: 2, of which 2 were waited for; matrix products, arithmetic and copies ran while one was open for 1% of the time, Pallas kernels for 29%

profile of v3, /device:TPU:0, one launch (start us, length us, event | category | flops | bytes accessed | tf_op | source)
XLA Modules:
  0.0 251.1 jit_solution(15129092085308021890)
XLA Ops:
  7.2 0.0 all-gather.6.cloned.1.call-start
  7.2 0.7 all-gather.6.cloned.1.call-update
  7.9 0.0 all-gather.4.cloned.1.call-start
  7.9 1.8 pad_maximum_fusion
  9.8 0.0 all-gather.4.cloned.1.call-update
  9.8 0.0 copy-start
  9.8 0.6 copy-done
  10.4 71.9 %shard_map.113 = bf16[32,4,32,512]{3,2,1,0:T(8,128)(2,1)} custom-call(s32[1,128]{1,0:T(1,128)S(1)} %bitcast.5, bf16[32,128256]{1,0:T(8,128)(2,1)} %table_ref.1), custom_call_target="tpu_custom_call" | custom-call | flops 60000002048 | bytes 8000000 | tf_op jit(solution)/shard_map/pallas_call | solution.py:163
  82.3 11.2 %all-gather.6.cloned.1.call-done = bf16[16384,256]{1,0:T(8,128)(2,1)} async-done(((bf16[512,256]{1,0:T(8,128)(2,1)}), bf16[16384,256]{1,0:T(8,128)(2,1)}) %all-gather.6.cloned.1.call-update) | async-done | bytes 8388624 | tf_op jit(solution)/shard_map/all_gather | solution.py:402
  93.5 78.6 %all-gather.4.cloned.1.call-done = bf16[8192,768]{1,0:T(8,128)(2,1)} async-done(((bf16[256,768]{1,0:T(8,128)(2,1)}), bf16[8192,768]{1,0:T(8,128)(2,1)}) %all-gather.4.cloned.1.call-update) | async-done | bytes 12582928 | tf_op jit(solution)/shard_map/all_gather | solution.py:400
  172.1 68.0 %shard_map.114 = (bf16[128,4096]{1,0:T(8,128)(2,1)}, bf16[1,2,512,256]{3,2,1,0:T(8,128)(2,1)}) custom-call(s32[32]{0:T(128)} %lens_ref.1, bf16[4096,512]{1,0:T(8,128)(2,1)} %bitcast.9, f32[1,4096]{1,0:T(1,128)} %bitcast.8, f32[512,128]{1,0:T(8,128)} %constant.4.clone.cos_ref, f32[512,128]{1,0:T(8,128)} %constant.5.clone.sin_ref, ...), custom_call_target="tpu_custom_call" | custom-call | flops 60000002048 | bytes 30000000 | tf_op jit(solution)/shard_map/pallas_call | solution.py:365
  240.1 2.3 copy.14
  242.4 1.9 copy.15
Async XLA Ops:
  7.2 86.3 %all-gather.6.cloned.1.call-start = ((), (), s32[]{:S(2)}) async-start(), calls=%async_computation.1 | async-start | bytes 8650752 | tf_op jit(solution)/shard_map/all_gather | solution.py:402
  7.9 164.2 %all-gather.4.cloned.1.call-start = ((), (), s32[]{:S(2)}) async-start(), calls=%async_computation | async-start | bytes 12976128 | tf_op jit(solution)/shard_map/all_gather | solution.py:400
  9.8 0.7 copy-start
Sparse Core Ops, SparseCore 0:
  9.7 83.7 all-gather.5
  95.8 76.2 all-gather.3

commit v4 on v3

--- a/solution.py
+++ b/solution.py
@@ -20,11 +20,145 @@
 BLOCKS = 252
 STRIP = BLOCKS * 128
 
+class Plane:
+    def __init__(self, whole, own, sems):
+        self.whole, self.own = whole, own
+        self.send, self.recv, self.core_send, self.core_recv = sems
+        self.z = lax.axis_index("z")
+        self.xlo = lax.axis_index("xlo")
+        self.core = lax.axis_index("core")
+        self.xhi = lax.axis_index("xhi")
+        self.y = lax.axis_index("y")
+        self.x = self.xhi * 2 + self.xlo
+        self.half = whole.shape[4] // 2
+
+    def neighbours(self):
+        found = []
+        for cls in range(2):
+            for way in range(2):
+                found.append(self.device(cls, self.first(cls) + (3 if way else 1), self.second(cls)))
+        found.append((self.z, self.xlo, 1 - self.core, self.xhi, self.y))
+        return found
+
+    def first(self, cls):
+        return self.x if cls else self.z
+
+    def second(self, cls):
+        return self.z if cls else self.x
+
+    def device(self, cls, f, s):
+        f, s = f % 4, s % 4
+        x, z = (f, s) if cls else (s, f)
+        return (z, x % 2, self.core, x // 2, self.y)
+
+    def rows(self, cls, part):
+        if part is None:
+            return pl.ds(cls * self.half, self.half)
+        return pl.ds(cls * self.half + part * (self.half // 2), self.half // 2)
+
+    def piece(self, cls, f, s, part=None):
+        f, s = f % 4, s % 4
+        x, z = (f, s) if cls else (s, f)
+        return self.whole.at[x // 2, z, x % 2, self.core, self.rows(cls, part)]
+
+    def copy(self, cls, stage, slot, f, s, part, own):
+        step = 3 if slot % 2 else 1
+        pf, ps = self.first(cls), self.second(cls)
+        to = self.device(cls, pf + step, ps) if stage == 0 else self.device(cls, pf, ps + step)
+        dst = self.piece(cls, f, s, part)
+        src = self.own.at[self.rows(cls, part)] if own else dst
+        return pltpu.make_async_remote_copy(
+            src, dst, self.send.at[cls, stage, slot], self.recv.at[cls, stage, slot], device_id=to, device_id_type=MESH
+        )
+
+    def full(self, cls, stage, way):
+        o = max(stage - 1, 0)
+        return self.copy(cls, stage, way, self.first(cls) + o, self.second(cls), None, o == 0)
+
+    def relay(self, cls, stage, way):
+        step = 1 if way else 3
+        f, s = self.first(cls), self.second(cls)
+        if stage == 0:
+            f = f + step
+        else:
+            f, s = f + stage - 1, s + step
+        return self.copy(cls, stage, 2 + way, f, s, way, False)
+
+    def cores(self, cls, o):
+        s = (self.second(cls) + o) % 4
+        if cls:
+            ref = self.whole.at[:, s, :, self.core, self.rows(cls, None)]
+        else:
+            ref = self.whole.at[s // 2, :, s % 2, self.core, self.rows(cls, None)]
+        return pltpu.make_async_remote_copy(
+            ref,
+            ref,
+            self.core_send.at[cls, o],
+            self.core_recv.at[cls, o],
+            device_id=(self.z, self.xlo, 1 - self.core, self.xhi, self.y),
+            device_id_type=MESH,
+        )
+
+    def each(self, act, *args):
+        for cls in range(2):
+            for way in range(2):
+                act(cls, way, *args)
+
+    def start_full(self, *stages):
+        for stage in stages:
+            self.each(lambda cls, way: self.full(cls, stage, way).start())
+
+    def take_full(self, *stages):
+        for stage in stages:
+            self.each(lambda cls, way: self.full(cls, stage, way).wait_recv())
+            self.each(lambda cls, way: self.relay(cls, stage, way).start())
+
+    def take_relay(self, *stages):
+        for stage in stages:
+            self.each(lambda cls, way: self.relay(cls, stage, way).wait_recv())
+
+    def step(self, n):
+        if n == 0:
+            self.start_full(0, 1)
+        elif n == 1:
+            self.take_full(0)
+            self.start_full(2, 4)
+        elif n == 2:
+            self.take_relay(0)
+            self.start_full(3)
+            self.take_full(1)
+        elif n == 3:
+            for cls in range(2):
+                self.cores(cls, 0).start()
+            self.take_full(2, 4)
+        elif n == 4:
+            self.take_full(3)
+            for o in (1, 3):
+                for cls in range(2):
+                    self.cores(cls, o).start()
+        elif n == 5:
+            self.take_relay(1, 2, 3, 4)
+            for cls in range(2):
+                self.cores(cls, 2).start()
+        else:
+            for cls in range(2):
+                for o in range(4):
+                    self.cores(cls, o).wait()
+            for stage in range(5):
+                self.each(lambda cls, way: self.full(cls, stage, way).wait_send())
+                self.each(lambda cls, way: self.relay(cls, stage, way).wait_send())
+
+    @staticmethod
+    def sems():
+        dma = pltpu.SemaphoreType.DMA
+        return [dma((2, 5, 4)), dma((2, 5, 4)), dma((2, 4)), dma((2, 4))]
+
+
 def place(g, y):
     return (g // 8, g // 4 % 2, g // 2 % 2, g % 2, y)
 
-def front_kernel(ids_ref, table_ref, out_ref, raw, major, rows, ids, spots, spots_s, stage,
-                 table_sems, spot_sem, id_send, id_recv, far_send, far_recv, side_send, side_recv):
+def front_kernel(ids_ref, table_ref, wq_ref, wk_ref, wv_ref, out_ref, whole_ref, raw, major, rows, ids, spots, spots_s, stage, own,
+                 table_sems, spot_sem, own_sems, id_send, id_recv, far_send, far_recv, side_send, side_recv, *plane_sems):
     feats, vocab = table_ref.shape
     z = lax.axis_index("z"); xlo = lax.axis_index("xlo"); core = lax.axis_index("core")
     xhi = lax.axis_index("xhi"); y = lax.axis_index("y")
@@ -32,6 +166,13 @@
     groups = out_ref.shape[0]
     up = (y + 1) % 4
     down = (y + 3) % 4
+    plane = Plane(whole_ref, own, plane_sems)
+    mine = [
+        pltpu.make_async_copy(ref, own.at[:, pl.ds(first, ref.shape[1])], own_sems.at[k])
+        for k, (ref, first) in enumerate(((wq_ref, 0), (wk_ref, 512), (wv_ref, 640)))
+    ]
+    for copy in mine:
+        copy.start()
     tiles = vocab // 128
     count = table_sems.shape[0]
     ends = [tiles * k // count for k in range(count + 1)]
@@ -54,8 +195,13 @@
     for k in range(1, 4):
         c = pltpu.make_async_remote_copy(ids_ref, ids.at[me, pl.ds(y, 1)], id_send.at[k - 1], id_recv.at[k - 1],
             device_id=place(me, (y + k) % 4), device_id_type=MESH)
-        c.start(); line.append(c)
-
+        c.start()
+        line.append(c)
+    for copy in mine:
+        copy.wait()
+    keep = pltpu.make_async_copy(own, whole_ref.at[xhi, z, xlo, core], own_sems.at[3])
+    keep.start()
+    plane.step(0)
     for copy in copies:
         copy.wait()
 
@@ -68,17 +214,23 @@
         major[pl.ds(pl.multiple_of(b * 128, 128), 128), :] = block.T.astype(jnp.float32)
         return 0
 
-    half = BLOCKS // 4
-    lax.fori_loop(0, half, turn, 0, unroll=9)
-    for c in line:
-        c.wait()
     def spread(k, _):
         to = (me + k) % groups
         pltpu.make_async_remote_copy(ids.at[me], ids.at[me], id_send.at[3], id_recv.at[3],
             device_id=place(to, y), device_id_type=MESH).start()
         return 0
-    lax.fori_loop(1, groups, spread, 0)
-    lax.fori_loop(half, BLOCKS, turn, 0, unroll=9)
+
+    for part in range(4):
+        lax.fori_loop(BLOCKS // 4 * part, BLOCKS // 4 * (part + 1), turn, 0, unroll=9)
+        if part == 0:
+            for c in line:
+                c.wait()
+            lax.fori_loop(1, groups, spread, 0)
+        elif part == 1:
+            plane.step(1)
+        elif part == 3:
+            plane.step(2)
+            keep.wait()
     others = pltpu.make_async_remote_copy(ids.at[pl.ds(0, groups - 1)], ids.at[pl.ds(0, groups - 1)], id_send.at[3], id_recv.at[3],
         device_id=place(me, up), device_id_type=MESH)
     others.wait_recv()
@@ -144,8 +296,11 @@
         side(p, 0, 0, 8, y, down, 1).start()
         if p:
             relay(p - 1)
+        if p < 3:
+            plane.step(3 + p)
     relay(3)
     others.wait_send()
+    plane.step(6)
     for p in range(4):
         n = 7 if p == 0 else 8
         pltpu.make_async_remote_copy(stage.at[p, pl.ds(0, n)], out_ref.at[pl.ds(0, n), y], far_send.at[p], far_recv.at[p],
@@ -158,13 +313,17 @@
         side(p, 0, 4, 4, up, down, 3).wait_send()
 
 
-def front(table, ids):
+def front(table, ids, wq, wk, wv):
     feats, vocab = table.shape
+    depth, across = wq.shape[0], wq.shape[1] + wk.shape[1] + wv.shape[1]
     return pl.pallas_call(
         front_kernel,
-        out_shape=jax.ShapeDtypeStruct((32, 4, feats, 512), jnp.bfloat16),
-        in_specs=[pl.BlockSpec(memory_space=pltpu.VMEM), pl.BlockSpec(memory_space=pl.ANY)],
-        out_specs=pl.BlockSpec(memory_space=pltpu.VMEM),
+        out_shape=(
+            jax.ShapeDtypeStruct((32, 4, feats, 512), jnp.bfloat16),
+            jax.ShapeDtypeStruct((2, 4, 2, 2, depth, across), jnp.bfloat16),
+        ),
+        in_specs=[pl.BlockSpec(memory_space=pltpu.VMEM)] + [pl.BlockSpec(memory_space=pl.ANY)] * 4,
+        out_specs=(pl.BlockSpec(memory_space=pltpu.VMEM), pl.BlockSpec(memory_space=pl.ANY)),
         scratch_shapes=[
             pltpu.VMEM((feats, vocab), jnp.bfloat16),
             pltpu.VMEM((STRIP, 128), jnp.float32),
@@ -173,23 +332,25 @@
             pltpu.VMEM((32, 4, 128), jnp.int32),
             pltpu.SMEM((32, 4, 128), jnp.int32),
             pltpu.VMEM((4, 8, feats, 512), jnp.bfloat16),
+            pltpu.VMEM((depth, across), jnp.bfloat16),
             pltpu.SemaphoreType.DMA((6,)),
             pltpu.SemaphoreType.DMA,
             pltpu.SemaphoreType.DMA((4,)),
             pltpu.SemaphoreType.DMA((4,)),
             pltpu.SemaphoreType.DMA((4,)),
             pltpu.SemaphoreType.DMA((4,)),
+            pltpu.SemaphoreType.DMA((4,)),
             pltpu.SemaphoreType.DMA((4, 4)),
             pltpu.SemaphoreType.DMA((4, 4)),
-        ],
+        ] + Plane.sems(),
         compiler_params=pltpu.CompilerParams(vmem_limit_bytes=50 * 2**20, collective_id=0, has_side_effects=True),
         cost_estimate=pl.CostEstimate(flops=60_000_000_000, bytes_accessed=8_000_000, transcendentals=0),
-    )(ids.reshape(1, 128), table)
+    )(ids.reshape(1, 128), table, wq, wk, wv)
 
 
 def back_kernel(lens_ref, tokens_ref, gain_ref, cos_ref, sin_ref, w_ref, wo_ref, hidden_ref, cache_ref,
                 turned, w, wo, x, normed, squares, q, k, v, attended, stage, mid, passed, final,
-                load_sems, far_send, far_recv, near_send, near_recv, sum_send, sum_recv):
+                load_sems, far_send, far_recv, near_send, near_recv, sum_send, sum_recv, *plane_sems):
     z = lax.axis_index("z"); xlo = lax.axis_index("xlo"); core = lax.axis_index("core")
     xhi = lax.axis_index("xhi"); y = lax.axis_index("y")
     me = ((z * 2 + xlo) * 2 + core) * 2 + xhi
@@ -205,14 +366,18 @@
     loads = [
         pltpu.make_async_copy(tokens_ref, turned, load_sems.at[0]),
         pltpu.make_async_copy(w_ref, w, load_sems.at[1]),
-        pltpu.make_async_copy(wo_ref, wo, load_sems.at[2]),
+        pltpu.make_async_copy(wo_ref, wo.at[xhi, z, xlo, core], load_sems.at[2]),
     ]
+    plane = Plane(wo, wo.at[xhi, z, xlo, core], plane_sems)
     for load in loads:
         load.start()
     barrier = pltpu.get_barrier_semaphore()
-    for member in (up, down):
-        pl.semaphore_signal(barrier, inc=1, device_id=at(member), device_id_type=MESH)
-    pl.semaphore_wait(barrier, 2)
+    greeted = [at(up), at(down)] + plane.neighbours()
+    for device in greeted:
+        pl.semaphore_signal(barrier, inc=1, device_id=device, device_id_type=MESH)
+    pl.semaphore_wait(barrier, len(greeted))
+    loads[2].wait()
+    plane.step(0)
 
     loads[0].wait()
     squares[...] = jnp.zeros_like(squares)
@@ -226,6 +391,7 @@
         return 0
 
     lax.fori_loop(0, width // 128, turn, 0, unroll=2)
+    plane.step(1)
     scale = lax.rsqrt(jnp.sum(squares[...], axis=1, keepdims=True) / width + norm_eps)
     squares[...] = jnp.broadcast_to(scale, squares.shape)
 
@@ -237,6 +403,7 @@
 
     lax.fori_loop(0, width // 128, norm, 0, unroll=2)
     loads[1].wait()
+    plane.step(2)
 
     def rotated(part):
         return (part * cos_ref[...] + pltpu.roll(part, HD // 2, 1) * sin_ref[...]).astype(jnp.bfloat16)
@@ -249,7 +416,10 @@
             q[pl.ds(i * 2 + h, 1)] = rotated(both[:, h * HD : (h + 1) * HD])[None]
         return 0
 
-    lax.fori_loop(0, 4, query, 0)
+    lax.fori_loop(0, 2, query, 0)
+    plane.step(3)
+    lax.fori_loop(2, 4, query, 0)
+    plane.step(4)
 
     for b in range(2):
         both = jnp.dot(normed[...], w[b, :, 512:768], preferred_element_type=jnp.float32)
@@ -260,6 +430,7 @@
         cache_ref[0, 0, :, b * HD : (b + 1) * HD] = key
         cache_ref[0, 1, :, b * HD : (b + 1) * HD] = value
 
+    plane.step(5)
     length = lens_ref[me]
 
     def head(h, _):
@@ -279,7 +450,7 @@
         return 0
 
     lax.fori_loop(0, 8, head, 0)
-    loads[2].wait()
+    plane.step(6)
 
     def send(src, dst, ssem, rsem, member):
         return pltpu.make_async_remote_copy(src, dst, ssem, rsem, device_id=at(member), device_id_type=MESH)
@@ -316,8 +487,8 @@
 
     def project(c, _):
         for half in range(2):
-            part = jnp.dot(attended[:, :512], wo[0, c * 2 + half], preferred_element_type=jnp.float32)
-            part = part + jnp.dot(attended[:, 512:], wo[1, c * 2 + half], preferred_element_type=jnp.float32)
+            part = jnp.dot(attended[:, :512], wo[0, c // 2, c % 2, half], preferred_element_type=jnp.float32)
+            part = part + jnp.dot(attended[:, 512:], wo[1, c // 2, c % 2, half], preferred_element_type=jnp.float32)
             part = part.astype(jnp.bfloat16)
             for member in range(4):
                 stage[pl.ds(c, 1), member, half] = part[member * quarter : (member + 1) * quarter][None]
@@ -373,7 +544,7 @@
         scratch_shapes=[
             pltpu.VMEM((width, prompt), bf),
             pltpu.VMEM(w.shape, bf),
-            pltpu.VMEM(wo.shape, bf),
+            pltpu.VMEM((2, 4, 2, 2, *wo.shape), bf),
             pltpu.VMEM((prompt, width), bf),
             pltpu.VMEM((prompt, width), bf),
             pltpu.VMEM((prompt, 128), jnp.float32),
@@ -386,7 +557,7 @@
             pltpu.VMEM((chunks, 2, quarter, 256), bf),
             pltpu.VMEM((chunks, 2, 2, quarter, 256), bf),
             dma((3,)),
-        ] + [dma((chunks, 2))] * 6,
+        ] + [dma((chunks, 2))] * 6 + Plane.sems(),
         compiler_params=pltpu.CompilerParams(vmem_limit_bytes=58 * 2**20, collective_id=1, has_side_effects=True),
         cost_estimate=pl.CostEstimate(flops=60_000_000_000, bytes_accessed=30_000_000, transcendentals=0),
     )(lengths, tokens, gain.reshape(1, width), cosine, sine, w, wo)
@@ -395,14 +566,10 @@
 def shards(prompt_ids, prompt_lengths, embed_table, norm_gain, w_query, w_key, w_value, w_out):
     row_count = prompt_ids.shape[0] * TPG
     model_width = embed_table.shape[0] * lax.axis_size(AXES)
-    packed = jnp.concatenate([w_query, w_key, w_value], axis=1)
-    plane = ("xhi", "z", "xlo", "core")
-    wide = lax.all_gather(packed, plane, axis=0, tiled=True)
-    wide = wide.reshape(2, model_width, packed.shape[1])
-    out_wide = lax.all_gather(w_out, plane, axis=0, tiled=False)
-    out_wide = out_wide.reshape(2, -1, *w_out.shape)
-    tokens = front(embed_table, prompt_ids).reshape(model_width, row_count)
-    return back(prompt_lengths, tokens, norm_gain, wide, out_wide)
+    tokens, wide = front(embed_table, prompt_ids, w_query, w_key, w_value)
+    tokens = tokens.reshape(model_width, row_count)
+    wide = wide.reshape(2, model_width, wide.shape[-1])
+    return back(prompt_lengths, tokens, norm_gain, wide, w_out)
 
 
 def solution(mesh):

time: 252 us -> 178 us (0.71)
  waiting for transfers between devices: 90.5 us -> 0 us
  Pallas kernels: 140 us -> 170 us
  between operations: 14.1 us -> 0.66 us
  local copies, waits for them, and re-layouts: 4.81 us -> 7.43 us
    all_gather x2 -> x0, waiting for transfers between devices: 89.8 us -> none  [the longest x1 78.6 us: shards(): wide = lax.all_gather(packed, plane, axis=0, tiled=True)]
    pallas_call x1, Pallas kernels: 71.9 us -> 87.2 us  [front(): pl.pallas_call(front_kernel, out_shape=(jax.ShapeDtypeStruct((32, 4, feat...]
    pallas_call x1, Pallas kernels: 68 us -> 82.6 us  [back(): pl.pallas_call(back_kernel, out_shape=(jax.ShapeDtypeStruct((quarter, wid...]
    unnamed x4 -> x10, local copies, waits for them, and re-layouts: 4.81 us -> 7.43 us
  transfers between devices with their start and end apart: 2 -> 0, of which waited for: 2 -> 0; matrix products, arithmetic and copies ran while one was open for 1% -> 0% of each run, Pallas kernels for 29% -> 0%
where the time goes in v4:
time: 178 us
  Pallas kernels  170 us (96%)
  local copies, waits for them, and re-layouts  7.43 us (4%)
    pallas_call x1, Pallas kernels, front(): pl.pallas_call(front_kernel, out_shape=(jax.ShapeDtypeStruct((32, 4, feat...  87.2 us
    pallas_call x1, Pallas kernels, back(): pl.pallas_call(back_kernel, out_shape=(jax.ShapeDtypeStruct((quarter, wid...  82.6 us
    unnamed x10, local copies, waits for them, and re-layouts  7.43 us

profile of v4, /device:TPU:0, one launch (start us, length us, event | category | flops | bytes accessed | tf_op | source)
XLA Modules:
  0.0 177.9 jit_solution(2356567311331702868)
XLA Ops:
  0.6 0.0 copy-start
  0.6 0.9 copy-done
  1.6 0.0 copy-start.1
  1.6 0.8 copy-done.1
  2.4 0.0 copy-start.2
  2.4 0.8 copy-done.2
  3.3 0.0 copy-start.3
  3.3 0.7 copy-done.3
  3.9 87.2 %shard_map.113 = (bf16[32,4,32,512]{3,2,1,0:T(8,128)(2,1)}, bf16[2,4,2,2,256,768]{5,4,3,2,1,0:T(8,128)(2,1)}) custom-call(s32[1,128]{1,0:T(1,128)S(1)} %bitcast.4, bf16[32,128256]{1,0:T(8,128)(2,1)} %table_ref.1, bf16[256,512]{1,0:T(8,128)(2,1)S(1)} %copy-done, bf16[256,128]{1,0:T(8,128)(2,1)S(1)} %copy-done.1, bf16[256,128]{1,0:T(8,128)(2,1)S(1)} %copy-done.2), custom_call_target="tpu_custom_call" | custom-call | flops 60000002048 | bytes 8000000 | tf_op jit(solution)/shard_map/pallas_call | solution.py:319
  91.1 82.6 %shard_map.114 = (bf16[128,4096]{1,0:T(8,128)(2,1)}, bf16[1,2,512,256]{3,2,1,0:T(8,128)(2,1)}) custom-call(s32[32]{0:T(128)} %lens_ref.1, bf16[4096,512]{1,0:T(8,128)(2,1)} %bitcast.7, f32[1,4096]{1,0:T(1,128)} %bitcast.5, f32[512,128]{1,0:T(8,128)} %constant.4.clone.cos_ref, f32[512,128]{1,0:T(8,128)} %constant.5.clone.sin_ref, ...), custom_call_target="tpu_custom_call" | custom-call | flops 60000002048 | bytes 30000000 | tf_op jit(solution)/shard_map/pallas_call | solution.py:536
  173.8 2.3 %copy.14 = bf16[128,4096]{1,0:T(8,128)(2,1)} copy(bf16[128,4096]{1,0:T(8,128)(2,1)} %get-tuple-element.8) | data formatting | bytes 2097152
  176.1 1.9 %copy.15 = bf16[1,2,512,256]{3,2,1,0:T(8,128)(2,1)} copy(bf16[1,2,512,256]{3,2,1,0:T(8,128)(2,1)} %get-tuple-element.9) | data formatting | bytes 1048576
Async XLA Ops:
  0.6 1.0 copy-start
  1.6 0.8 copy-start.1
  2.4 0.8 copy-start.2
  3.3 0.7 copy-start.3

commit v5 on v4

v5 whole, which is shorter than its diff:
```python
import jax
import jax.numpy as jnp
import numpy as np
from jax import lax
from jax.experimental import pallas as pl
from jax.experimental.pallas import tpu as pltpu
from jax.sharding import Mesh
from jax.sharding import PartitionSpec as P

HD = 128
AXES = ("z", "xlo", "core", "xhi", "y")
DP = ("z", "xlo", "core")
TENSOR = ("xhi", "y")
MESH = pl.DeviceIdType.MESH

norm_eps = 1e-05
rope_theta = 500000.0

BLOCKS = 252
STRIP = BLOCKS * 128
TILES = 21
LOADS = BLOCKS // TILES


class Plane:
    def __init__(self, whole, own, sems):
        self.whole, self.own = whole, own
        self.send, self.recv, self.core_send, self.core_recv = sems
        self.z = lax.axis_index("z")
        self.xlo = lax.axis_index("xlo")
        self.core = lax.axis_index("core")
        self.xhi = lax.axis_index("xhi")
        self.y = lax.axis_index("y")
        self.x = self.xhi * 2 + self.xlo
        self.half = whole.shape[4] // 2

    def neighbours(self):
        found = []
        for cls in range(2):
            for way in range(2):
                found.append(self.device(cls, self.first(cls) + (3 if way else 1), self.second(cls)))
        found.append((self.z, self.xlo, 1 - self.core, self.xhi, self.y))
        return found

    def first(self, cls):
        return self.x if cls else self.z

    def second(self, cls):
        return self.z if cls else self.x

    def device(self, cls, f, s):
        f, s = f % 4, s % 4
        x, z = (f, s) if cls else (s, f)
        return (z, x % 2, self.core, x // 2, self.y)

    def rows(self, cls, part):
        if part is None:
            return pl.ds(cls * self.half, self.half)
        return pl.ds(cls * self.half + part * (self.half // 2), self.half // 2)

    def piece(self, cls, f, s, part=None):
        f, s = f % 4, s % 4
        x, z = (f, s) if cls else (s, f)
        return self.whole.at[x // 2, z, x % 2, self.core, self.rows(cls, part)]

    def copy(self, cls, stage, slot, f, s, part, own):
        step = 3 if slot % 2 else 1
        pf, ps = self.first(cls), self.second(cls)
        to = self.device(cls, pf + step, ps) if stage == 0 else self.device(cls, pf, ps + step)
        dst = self.piece(cls, f, s, part)
        src = self.own.at[self.rows(cls, part)] if own else dst
        return pltpu.make_async_remote_copy(
            src, dst, self.send.at[cls, stage, slot], self.recv.at[cls, stage, slot], device_id=to, device_id_type=MESH
        )

    def full(self, cls, stage, way):
        o = max(stage - 1, 0)
        return self.copy(cls, stage, way, self.first(cls) + o, self.second(cls), None, o == 0)

    def relay(self, cls, stage, way):
        step = 1 if way else 3
        f, s = self.first(cls), self.second(cls)
        if stage == 0:
            f = f + step
        else:
            f, s = f + stage - 1, s + step
        return self.copy(cls, stage, 2 + way, f, s, way, False)

    def cores(self, cls, o):
        s = (self.second(cls) + o) % 4
        if cls:
            ref = self.whole.at[:, s, :, self.core, self.rows(cls, None)]
        else:
            ref = self.whole.at[s // 2, :, s % 2, self.core, self.rows(cls, None)]
        return pltpu.make_async_remote_copy(
            ref,
            ref,
            self.core_send.at[cls, o],
            self.core_recv.at[cls, o],
            device_id=(self.z, self.xlo, 1 - self.core, self.xhi, self.y),
            device_id_type=MESH,
        )

    def each(self, act, *args):
        for cls in range(2):
            for way in range(2):
                act(cls, way, *args)

    def start_full(self, *stages):
        for stage in stages:
            self.each(lambda cls, way: self.full(cls, stage, way).start())

    def take_full(self, *stages):
        for stage in stages:
            self.each(lambda cls, way: self.full(cls, stage, way).wait_recv())
            self.each(lambda cls, way: self.relay(cls, stage, way).start())

    def take_relay(self, *stages):
        for stage in stages:
            self.each(lambda cls, way: self.relay(cls, stage, way).wait_recv())

    def step(self, n):
        if n == 0:
            self.start_full(0, 1)
        elif n == 1:
            self.take_full(0)
            self.start_full(2, 4)
        elif n == 2:
            self.take_relay(0)
            self.start_full(3)
            self.take_full(1)
        elif n == 3:
            for cls in range(2):
                self.cores(cls, 0).start()
            self.take_full(2, 4)
        elif n == 4:
            self.take_full(3)
            for o in (1, 3):
                for cls in range(2):
                    self.cores(cls, o).start()
        elif n == 5:
            self.take_relay(1, 2, 3, 4)
            for cls in range(2):
                self.cores(cls, 2).start()
        else:
            for cls in range(2):
                for o in range(4):
                    self.cores(cls, o).wait()
            for stage in range(5):
                self.each(lambda cls, way: self.full(cls, stage, way).wait_send())
                self.each(lambda cls, way: self.relay(cls, stage, way).wait_send())

    @staticmethod
    def sems():
        dma = pltpu.SemaphoreType.DMA
        return [dma((2, 5, 4)), dma((2, 5, 4)), dma((2, 4)), dma((2, 4))]


def place(g, y):
    return (g // 8, g // 4 % 2, g // 2 % 2, g % 2, y)


def kernel(lens_ref, ids_ref, gain_ref, cos_ref, sin_ref, table_ref, wq_ref, wk_ref, wv_ref, wo_ref, hidden_ref, cache_ref,
           raw, major, rows, ids, spots, spots_s, staged, xt, w, wo, own_x, xb, normed, squares, q, k, v, attended,
           stage, mid, passed, final, table_sems, spot_sem, own_sems, id_send, id_recv, look_send, look_recv,
           side_send, side_recv, far_send, far_recv, near_send, near_recv, sum_send, sum_recv, *plane_sems):
    feats, vocab = table_ref.shape
    z = lax.axis_index("z")
    xlo = lax.axis_index("xlo")
    core = lax.axis_index("core")
    xhi = lax.axis_index("xhi")
    y = lax.axis_index("y")
    me = ((z * 2 + xlo) * 2 + core) * 2 + xhi
    groups = ids.shape[0]
    quarter, width = hidden_ref.shape
    up = (y + 1) % 4
    down = (y + 3) % 4
    far = (y + 2) % 4
    tiles = vocab // 128

    def at(member):
        return place(me, member)

    def send(src, dst, ssem, rsem, device):
        return pltpu.make_async_remote_copy(src, dst, ssem, rsem, device_id=device, device_id_type=MESH)


    def table_base(n, strip):
        return jnp.minimum(strip * BLOCKS + n * TILES, tiles - TILES)

    def table_copy(n, strip):
        first = pl.multiple_of(table_base(n, strip) * 128, 128)
        return pltpu.make_async_copy(
            table_ref.at[:, pl.ds(first, TILES * 128)], raw.at[n % 2, strip], table_sems.at[n % 2, strip]
        )

    for n in range(2):
        for strip in range(4):
            table_copy(n, strip).start()
    own_w = w.at[xhi, z, xlo, core]
    own_wo = wo.at[xhi, z, xlo, core]
    mine = [
        pltpu.make_async_copy(ref, own_w.at[:, pl.ds(first, ref.shape[1])], own_sems.at[n])
        for n, (ref, first) in enumerate(((wq_ref, 0), (wk_ref, 512), (wv_ref, 640)))
    ] + [pltpu.make_async_copy(wo_ref, own_wo, own_sems.at[3])]
    for copy in mine:
        copy.start()
    plane_w = Plane(w, own_w, plane_sems[:4])
    plane_o = Plane(wo, own_wo, plane_sems[4:])

    barrier = pltpu.get_barrier_semaphore()
    for n in range(1, 4):
        pl.semaphore_signal(barrier, inc=1, device_id=at((y + n) % 4), device_id_type=MESH)

    def greet(n, _):
        pl.semaphore_signal(barrier, inc=1, device_id=place((me + n) % groups, y), device_id_type=MESH)
        return 0

    lax.fori_loop(1, groups, greet, 0)

    def turn(n, _):
        for strip in range(4):
            table_copy(n, strip).wait()

        def tile(t, _):
            parts = []
            for strip in range(4):
                first = jnp.minimum(strip * BLOCKS + n * TILES + t, tiles - 1) - table_base(n, strip)
                parts.append(raw[n % 2, strip, :, pl.ds(pl.multiple_of(first * 128, 128), 128)])
            block = jnp.concatenate(parts, axis=0)
            major[pl.ds(pl.multiple_of((n * TILES + t) * 128, 128), 128), :] = block.T.astype(jnp.float32)
            return 0

        lax.fori_loop(0, TILES, tile, 0, unroll=7)

        @pl.when(n + 2 < LOADS)
        def _():
            for strip in range(4):
                table_copy(n + 2, strip).start()

        return 0

    lax.fori_loop(0, 3, turn, 0)
    pl.semaphore_wait(barrier, 3 + groups - 1)
    ids[pl.ds(me, 1), pl.ds(y, 1), :] = ids_ref[...][None]
    line = [
        send(ids_ref, ids.at[me, pl.ds(y, 1)], id_send.at[n - 1], id_recv.at[n - 1], at((y + n) % 4)) for n in range(1, 4)
    ]
    for copy in line:
        copy.start()
    for copy in mine:
        copy.wait()
    plane_w.step(0)
    lax.fori_loop(3, 6, turn, 0)
    for copy in line:
        copy.wait()

    def spread(n, _):
        send(ids.at[me], ids.at[me], id_send.at[3], id_recv.at[3], place((me + n) % groups, y)).start()
        return 0

    lax.fori_loop(1, groups, spread, 0)
    lax.fori_loop(6, 9, turn, 0)
    plane_w.step(1)
    lax.fori_loop(9, LOADS, turn, 0)
    most = pl.ds(0, groups - 1)
    others = send(ids.at[most], ids.at[most], id_send.at[3], id_recv.at[3], at(up))
    others.wait_recv()
    all_ids = ids[...]
    strip_of = jnp.zeros_like(all_ids)
    for n in range(1, 4):
        strip_of = strip_of + jnp.where(all_ids >= n * STRIP, 1, 0)
    spots[...] = all_ids - strip_of * STRIP
    to_smem = pltpu.make_async_copy(spots, spots_s, spot_sem)
    to_smem.start()
    to_smem.wait()
    eye = (
        lax.broadcasted_iota(jnp.int32, (128, 128), 0) == lax.broadcasted_iota(jnp.int32, (128, 128), 1)
    ).astype(jnp.bfloat16)


    def look(s):
        def four(j, _):
            def some(i, _):
                g = (me + 4 * j + i) % groups
                for n in range(128):
                    rows[pl.ds(i * 128 + n, 1), :] = major[pl.ds(spots_s[g, s, n], 1), :]
                return 0

            lax.fori_loop(0, 4, some, 0)
            found = lax.dot_general(
                eye, rows[...].astype(jnp.bfloat16), (((1,), (1,)), ((), ())), preferred_element_type=jnp.float32
            )
            for i in range(4):
                g = (me + 4 * j + i) % groups
                word = ids[pl.ds(g, 1), pl.ds(s, 1), :].reshape(1, 128)
                part = found[:, i * 128 : (i + 1) * 128]
                chosen = part[:feats]
                for n in range(1, 4):
                    chosen = jnp.where(word >= n * STRIP, part[n * feats : (n + 1) * feats], chosen)
                chosen = chosen.astype(jnp.bfloat16)
                staged[s, pl.ds(4 * j + i, 1)] = chosen[None]

                def give():
                    send(staged.at[s, 4 * j + i], xt.at[s, me, y], look_send.at[s], look_recv.at[s], place(g, y)).start()

                if i:
                    give()
                else:
                    pl.when(j > 0)(give)

                    @pl.when(j == 0)
                    def _():
                        xt[s, pl.ds(me, 1), pl.ds(y, 1)] = chosen[None, None]

            return 0

        lax.fori_loop(0, 8, four, 0)

    def looked(s):
        return send(staged.at[s, most], xt.at[s, most, y], look_send.at[s], look_recv.at[s], at(up))

    def side(s, slot):
        first, count, of = ((0, groups, y), (0, groups, y), (0, groups // 2, down), (groups // 2, groups // 2, up))[slot]
        part = xt.at[s, pl.ds(first, count), of]
        return send(part, part, side_send.at[s, slot], side_recv.at[s, slot], at(down if slot % 2 else up))

    def gather(s):
        looked(s).wait_recv()
        side(s, 0).start()
        side(s, 1).start()

    def relay(s):
        for way in range(2):
            side(s, way).wait_recv()
            side(s, 2 + way).start()


    length = lens_ref[me]

    def block(s):
        for way in range(2):
            side(s, 2 + way).wait_recv()
        squares[...] = jnp.zeros_like(squares)

        def over(c, _):
            cols = pl.ds(pl.multiple_of(c * 128, 128), 128)
            piece = xt[s, pl.ds(c, 1)].reshape(128, 128).T
            xb[:, cols] = piece
            wide = piece.astype(jnp.float32)
            squares[...] += wide * wide
            return 0

        lax.fori_loop(0, width // 128, over, 0, unroll=4)
        scale = lax.rsqrt(jnp.sum(squares[...], axis=1, keepdims=True) / width + norm_eps)
        squares[...] = jnp.broadcast_to(scale, squares.shape)

        @pl.when(y == s)
        def _():
            own_x[...] = xb[...]

        def norm(c, _):
            cols = pl.ds(pl.multiple_of(c * 128, 128), 128)
            wide = xb[:, cols].astype(jnp.float32) * squares[...] * gain_ref[:, cols]
            normed[:, cols] = wide.astype(jnp.bfloat16)
            return 0

        lax.fori_loop(0, width // 128, norm, 0, unroll=4)
        here = slice(s * quarter, (s + 1) * quarter)

        def project(b, first):
            return jnp.dot(
                normed[...],
                w[b, :, :, :, :, first : first + 256].reshape(width, 256),
                preferred_element_type=jnp.float32,
            )

        def rotated(part):
            return (part * cos_ref[here, :] + pltpu.roll(part, HD // 2, 1) * sin_ref[here, :]).astype(jnp.bfloat16)

        def heads(b, _):
            for n in range(2):
                both = project(b, n * 256)
                for h in range(2):
                    q[pl.ds(b * 4 + n * 2 + h, 1)] = rotated(both[:, h * HD : (h + 1) * HD])[None]
            both = project(b, 512)
            k[pl.ds(b, 1), here] = rotated(both[:, :HD])[None]
            v[pl.ds(b, 1), here] = both[:, HD:].astype(jnp.bfloat16)[None]
            return 0

        lax.fori_loop(0, 2, heads, 0)
        for b in range(2):
            cache_ref[0, 0, here, b * HD : (b + 1) * HD] = k[b, here]
            cache_ref[0, 1, here, b * HD : (b + 1) * HD] = v[b, here]
        keys = (s + 1) * quarter
        p = lax.broadcasted_iota(jnp.int32, (quarter, keys), 0) + s * quarter
        j = lax.broadcasted_iota(jnp.int32, (quarter, keys), 1)
        allowed = (j <= p) & (j < length)

        def head(h, _):
            b = h // 4
            scores = lax.dot_general(
                q[h], k[b, :keys], (((1,), (1,)), ((), ())), preferred_element_type=jnp.float32
            )
            scores = jnp.where(allowed, scores * np.float32(1 / np.sqrt(HD)), -1e30)
            expd = jnp.exp(scores - jnp.max(scores, axis=1, keepdims=True))
            weights = (expd / jnp.sum(expd, axis=1, keepdims=True)).astype(jnp.bfloat16)
            got = jnp.dot(weights, v[b, :keys], preferred_element_type=jnp.float32)
            attended[here, pl.ds(pl.multiple_of(h * HD, HD), HD)] = got.astype(jnp.bfloat16)
            return 0

        lax.fori_loop(0, 8, head, 0, unroll=2)

    look(0)
    plane_w.step(2)
    look(1)
    gather(0)
    look(2)
    gather(1)
    relay(0)
    plane_w.step(3)
    look(3)
    gather(2)
    relay(1)
    plane_w.step(4)
    gather(3)
    plane_o.step(0)
    plane_w.step(5)
    plane_w.step(6)
    relay(2)
    block(0)
    relay(3)
    plane_o.step(1)
    block(1)
    plane_o.step(2)
    block(2)
    plane_o.step(3)
    plane_o.step(4)
    block(3)
    plane_o.step(5)
    others.wait_send()
    for s in range(4):
        looked(s).wait_send()
        for slot in range(4):
            side(s, slot).wait_send()
    plane_o.step(6)


    def far_copy(c, way):
        return send(stage.at[c, far, way], mid.at[c, way], far_send.at[c, way], far_recv.at[c, way], at(down if way else up))

    def near_copy(c, way):
        part = stage.at[c, down if way else up, 1 - way]
        return send(part, final.at[c, way, 1 - way], near_send.at[c, way], near_recv.at[c, way], at(down if way else up))

    def sum_copy(c, way):
        return send(passed.at[c, way], final.at[c, way, way], sum_send.at[c, way], sum_recv.at[c, way], at(down if way else up))

    def wide(ref):
        return ref.reshape(quarter, 256).astype(jnp.float32)

    def pass_on(c):
        for way in range(2):
            far_copy(c, way).wait_recv()
            total = wide(stage[pl.ds(c, 1), pl.ds(down if way else up, 1), way]) + wide(mid[pl.ds(c, 1), way])
            passed[pl.ds(c, 1), way] = total.astype(jnp.bfloat16)[None]
            sum_copy(c, way).start()

    def finish(c, _):
        for way in range(2):
            near_copy(c, way).wait_recv()
            sum_copy(c, way).wait_recv()
        for half in range(2):
            cols = pl.ds(pl.multiple_of(c * 512 + half * 256, 256), 256)
            total = wide(stage[pl.ds(c, 1), pl.ds(y, 1), half])
            for way in range(2):
                total = total + wide(final[pl.ds(c, 1), way, half])
            hidden_ref[:, cols] = (own_x[:, cols].astype(jnp.float32) + total).astype(jnp.bfloat16)
        return 0

    chunks = stage.shape[0]

    def output(c, _):
        for half in range(2):
            part = jnp.dot(attended[:, :512], wo[0, c // 2, c % 2, half], preferred_element_type=jnp.float32)
            part = part + jnp.dot(attended[:, 512:], wo[1, c // 2, c % 2, half], preferred_element_type=jnp.float32)
            part = part.astype(jnp.bfloat16)
            for member in range(4):
                stage[pl.ds(c, 1), member, half] = part[member * quarter : (member + 1) * quarter][None]
        for way in range(2):
            far_copy(c, way).start()
        for way in range(2):
            near_copy(c, way).start()

        @pl.when(c > 0)
        def _():
            pass_on(c - 1)

        return 0

    lax.fori_loop(0, chunks, output, 0)
    pass_on(chunks - 1)
    lax.fori_loop(0, chunks, finish, 0)

    def drain(c, _):
        for way in range(2):
            far_copy(c, way).wait_send()
            near_copy(c, way).wait_send()
            sum_copy(c, way).wait_send()
        return 0

    lax.fori_loop(0, chunks, drain, 0)


def shards(prompt_ids, prompt_lengths, embed_table, norm_gain, w_query, w_key, w_value, w_out):
    quarter = prompt_ids.shape[0]
    prompt = quarter * 4
    feats, vocab = embed_table.shape
    width = feats * lax.axis_size(AXES)
    depth, across = w_query.shape[0], w_query.shape[1] + w_key.shape[1] + w_value.shape[1]
    groups = prompt_lengths.shape[0]
    angle = np.arange(prompt)[:, None] * rope_theta ** (-2.0 * np.arange(HD // 2) / HD)[None, :]
    cosine = np.concatenate([np.cos(angle), np.cos(angle)], axis=1).astype(np.float32)
    sine = np.concatenate([-np.sin(angle), np.sin(angle)], axis=1).astype(np.float32)
    chunks = width // 512
    bf, f32 = jnp.bfloat16, jnp.float32
    vmem = pl.BlockSpec(memory_space=pltpu.VMEM)
    anyw = pl.BlockSpec(memory_space=pl.ANY)
    dma = pltpu.SemaphoreType.DMA
    return pl.pallas_call(
        kernel,
        out_shape=(
            jax.ShapeDtypeStruct((quarter, width), bf),
            jax.ShapeDtypeStruct((1, 2, prompt, 2 * HD), bf),
        ),
        in_specs=[pl.BlockSpec(memory_space=pltpu.SMEM)] + [vmem] * 4 + [anyw] * 5,
        out_specs=(vmem, vmem),
        scratch_shapes=[
            pltpu.VMEM((2, 4, feats, TILES * 128), bf),
            pltpu.VMEM((STRIP, 128), f32),
            pltpu.VMEM((512, 128), f32),
            pltpu.VMEM((groups, 4, 128), jnp.int32),
            pltpu.VMEM((groups, 4, 128), jnp.int32),
            pltpu.SMEM((groups, 4, 128), jnp.int32),
            pltpu.VMEM((4, groups, feats, 128), bf),
            pltpu.VMEM((4, groups, 4, feats, 128), bf),
            pltpu.VMEM((2, 4, 2, 2, depth, across), bf),
            pltpu.VMEM((2, 4, 2, 2, *w_out.shape), bf),
            pltpu.VMEM((quarter, width), bf),
            pltpu.VMEM((quarter, width), bf),
            pltpu.VMEM((quarter, width), bf),
            pltpu.VMEM((quarter, 128), f32),
            pltpu.VMEM((8, quarter, HD), bf),
            pltpu.VMEM((2, prompt, HD), bf),
            pltpu.VMEM((2, prompt, HD), bf),
            pltpu.VMEM((prompt, 1024), bf),
            pltpu.VMEM((chunks, 4, 2, quarter, 256), bf),
            pltpu.VMEM((chunks, 2, quarter, 256), bf),
            pltpu.VMEM((chunks, 2, quarter, 256), bf),
            pltpu.VMEM((chunks, 2, 2, quarter, 256), bf),
            dma((2, 4)),
            dma,
            dma((4,)),
            dma((4,)),
            dma((4,)),
            dma((4,)),
            dma((4,)),
            dma((4, 4)),
            dma((4, 4)),
        ]
        + [dma((chunks, 2))] * 6
        + Plane.sems()
        + Plane.sems(),
        compiler_params=pltpu.CompilerParams(vmem_limit_bytes=67043328, collective_id=0, has_side_effects=True),
    )(
        prompt_lengths,
        prompt_ids.reshape(1, quarter),
        norm_gain.reshape(1, width),
        cosine,
        sine,
        embed_table,
        w_query,
        w_key,
        w_value,
        w_out,
    )


def solution(mesh):
    split = Mesh(mesh.devices.reshape(4, 2, 2, 2, 4), AXES)
    placed = (
        P(AXES),
        P(),
        P(AXES, None),
        P(),
        P(DP, TENSOR),
        P(DP, TENSOR),
        P(DP, TENSOR),
        P(TENSOR, DP),
    )
    return jax.shard_map(
        shards,
        mesh=split,
        in_specs=placed,
        out_specs=(P(AXES, None), P(AXES, None, None, None)),
        check_vma=False,
    )
```

time: 178 us -> 141 us (0.79)
  Pallas kernels: 170 us -> 136 us
  local copies, waits for them, and re-layouts: 7.43 us -> 4.16 us
    pallas_call x2 -> x1, Pallas kernels: 170 us -> 136 us  [shards(): pl.pallas_call(kernel, out_shape=(jax.ShapeDtypeStruct((quarter, width),...]
    unnamed x10 -> x2, local copies, waits for them, and re-layouts: 7.43 us -> 4.16 us
where the time goes in v5:
time: 141 us; the launch traced here: 140 us
  Pallas kernels  136 us (96%)
  local copies, waits for them, and re-layouts  4.16 us (3%)
    pallas_call x1, Pallas kernels, shards(): pl.pallas_call(kernel, out_shape=(jax.ShapeDtypeStruct((quarter, width),...  136 us
    unnamed x2, local copies, waits for them, and re-layouts  4.16 us

profile of v5, /device:TPU:0, one launch (start us, length us, event | category | flops | bytes accessed | tf_op | source)
XLA Modules:
  0.0 140.5 jit_solution(15224106419971539423)
XLA Ops:
  0.6 135.7 %shard_map.113 = (bf16[128,4096]{1,0:T(8,128)(2,1)}, bf16[1,2,512,256]{3,2,1,0:T(8,128)(2,1)}) custom-call(s32[32]{0:T(128)} %lens_ref.1, s32[1,128]{1,0:T(1,128)} %bitcast.3, f32[1,4096]{1,0:T(1,128)} %bitcast.2, f32[512,128]{1,0:T(8,128)} %constant.4.clone.cos_ref, f32[512,128]{1,0:T(8,128)} %constant.5.clone.sin_ref, bf16[32,128256]{1,0:T(8,128)(2,1)} %table_ref.1, ...), custom_call_target="tpu_custom_call" | custom-call | tf_op jit(solution)/shard_map/pallas_call | solution.py:530
  136.3 2.3 %copy.14 = bf16[128,4096]{1,0:T(8,128)(2,1)} copy(bf16[128,4096]{1,0:T(8,128)(2,1)} %get-tuple-element.4) | data formatting | bytes 2097152
  138.6 1.9 %copy.15 = bf16[1,2,512,256]{3,2,1,0:T(8,128)(2,1)} copy(bf16[1,2,512,256]{3,2,1,0:T(8,128)(2,1)} %get-tuple-element.5) | data formatting | bytes 1048576

commit v6 on v5

--- a/solution.py
+++ b/solution.py
@@ -23,8 +23,8 @@
 
 
 class Plane:
-    def __init__(self, whole, own, sems):
-        self.whole, self.own = whole, own
+    def __init__(self, whole, own, sems, by_row=False):
+        self.whole, self.own, self.by_row = whole, own, by_row
         self.send, self.recv, self.core_send, self.core_recv = sems
         self.z = lax.axis_index("z")
         self.xlo = lax.axis_index("xlo")
@@ -87,8 +87,8 @@
         return self.copy(cls, stage, 2 + way, f, s, way, False)
 
     def cores(self, cls, o):
-        s = (self.second(cls) + o) % 4
-        if cls:
+        s = ((self.z if self.by_row else self.second(cls)) + o) % 4
+        if cls or self.by_row:
             ref = self.whole.at[:, s, :, self.core, self.rows(cls, None)]
         else:
             ref = self.whole.at[s // 2, :, s % 2, self.core, self.rows(cls, None)]
@@ -119,12 +119,79 @@
         for stage in stages:
             self.each(lambda cls, way: self.relay(cls, stage, way).wait_recv())
 
-    def step(self, n):
+    def start_cores(self, cls, *offsets):
+        for o in offsets:
+            self.cores(cls, o).start()
+
+    def row_step(self, n):
+        ways = range(2)
         if n == 0:
             self.start_full(0, 1)
         elif n == 1:
             self.take_full(0)
             self.start_full(2, 4)
+        elif n == 2:
+            self.take_relay(0)
+            self.start_full(3)
+            self.take_full(1)
+            self.start_cores(1, 0)
+        elif n == 3:
+            for way in ways:
+                self.relay(0, 1, way).wait_recv()
+            self.start_cores(0, 0)
+            self.take_full(2, 4)
+        elif n == 4:
+            self.take_full(3)
+            self.start_cores(1, 1, 3)
+            for stage in (2, 4):
+                for way in ways:
+                    self.relay(0, stage, way).wait_recv()
+            self.start_cores(0, 1, 3)
+        else:
+            for way in ways:
+                self.relay(0, 3, way).wait_recv()
+                for stage in range(1, 5):
+                    self.relay(1, stage, way).wait_recv()
+            self.start_cores(0, 2)
+            self.start_cores(1, 2)
+
+    def row_ready(self, o):
+        for cls in range(2):
+            self.cores(cls, o).wait_recv()
+
+    def drain(self):
+        for cls in range(2):
+            for o in range(4):
+                self.cores(cls, o).wait_send()
+        for stage in range(5):
+            self.each(lambda cls, way: self.full(cls, stage, way).wait_send())
+            self.each(lambda cls, way: self.relay(cls, stage, way).wait_send())
+
+    def step(self, n):
+        if n == 0:
+            self.start_full(1)
+        elif n == -1:
+            self.start_full(0)
+        elif n == 1:
+            self.take_full(0)
+            self.start_full(2, 4)
+        elif n == 10:
+            self.take_full(0)
+        elif n == 11:
+            self.start_full(2)
+        elif n == 12:
+            self.start_full(4)
+        elif n == 13:
+            self.take_relay(0)
+            self.start_full(3)
+        elif n == 14:
+            self.take_full(1)
+        elif n == 15:
+            for cls in range(2):
+                self.cores(cls, 0).start()
+            self.take_full(2)
+        elif n == 16:
+            self.take_full(4)
         elif n == 2:
             self.take_relay(0)
             self.start_full(3)
@@ -145,10 +212,7 @@
         else:
             for cls in range(2):
                 for o in range(4):
-                    self.cores(cls, o).wait()
-            for stage in range(5):
-                self.each(lambda cls, way: self.full(cls, stage, way).wait_send())
-                self.each(lambda cls, way: self.relay(cls, stage, way).wait_send())
+                    self.cores(cls, o).wait_recv()
 
     @staticmethod
     def sems():
@@ -184,6 +248,16 @@
     def send(src, dst, ssem, rsem, device):
         return pltpu.make_async_remote_copy(src, dst, ssem, rsem, device_id=device, device_id_type=MESH)
 
+    barrier = pltpu.get_barrier_semaphore()
+    for n in range(1, 4):
+        pl.semaphore_signal(barrier, inc=1, device_id=at((y + n) % 4), device_id_type=MESH)
+
+    def greet(n, _):
+        pl.semaphore_signal(barrier, inc=1, device_id=place((me + n) % groups, y), device_id_type=MESH)
+        return 0
+
+    lax.fori_loop(1, groups, greet, 0)
+
 
     def table_base(n, strip):
         return jnp.minimum(strip * BLOCKS + n * TILES, tiles - TILES)
@@ -206,17 +280,7 @@
     for copy in mine:
         copy.start()
     plane_w = Plane(w, own_w, plane_sems[:4])
-    plane_o = Plane(wo, own_wo, plane_sems[4:])
-
-    barrier = pltpu.get_barrier_semaphore()
-    for n in range(1, 4):
-        pl.semaphore_signal(barrier, inc=1, device_id=at((y + n) % 4), device_id_type=MESH)
-
-    def greet(n, _):
-        pl.semaphore_signal(barrier, inc=1, device_id=place((me + n) % groups, y), device_id_type=MESH)
-        return 0
-
-    lax.fori_loop(1, groups, greet, 0)
+    plane_o = Plane(wo, own_wo, plane_sems[4:], True)
 
     def turn(n, _):
         for strip in range(4):
@@ -240,7 +304,7 @@
 
         return 0
 
-    lax.fori_loop(0, 3, turn, 0)
+    lax.fori_loop(0, 2, turn, 0)
     pl.semaphore_wait(barrier, 3 + groups - 1)
     ids[pl.ds(me, 1), pl.ds(y, 1), :] = ids_ref[...][None]
     line = [
@@ -250,8 +314,8 @@
         copy.start()
     for copy in mine:
         copy.wait()
-    plane_w.step(0)
-    lax.fori_loop(3, 6, turn, 0)
+    plane_w.step(-1)
+    lax.fori_loop(2, 5, turn, 0)
     for copy in line:
         copy.wait()
 
@@ -260,9 +324,8 @@
         return 0
 
     lax.fori_loop(1, groups, spread, 0)
-    lax.fori_loop(6, 9, turn, 0)
-    plane_w.step(1)
-    lax.fori_loop(9, LOADS, turn, 0)
+    plane_w.step(0)
+    lax.fori_loop(5, LOADS, turn, 0)
     most = pl.ds(0, groups - 1)
     others = send(ids.at[most], ids.at[most], id_send.at[3], id_recv.at[3], at(up))
     others.wait_recv()
@@ -270,21 +333,25 @@
     strip_of = jnp.zeros_like(all_ids)
     for n in range(1, 4):
         strip_of = strip_of + jnp.where(all_ids >= n * STRIP, 1, 0)
-    spots[...] = all_ids - strip_of * STRIP
-    to_smem = pltpu.make_async_copy(spots, spots_s, spot_sem)
-    to_smem.start()
-    to_smem.wait()
+    spots_of = all_ids - strip_of * STRIP
+    for s in range(4):
+        spots[s] = spots_of[:, s]
+    to_smem = [pltpu.make_async_copy(spots.at[s], spots_s.at[s], spot_sem.at[s]) for s in range(4)]
+    for copy in to_smem:
+        copy.start()
     eye = (
         lax.broadcasted_iota(jnp.int32, (128, 128), 0) == lax.broadcasted_iota(jnp.int32, (128, 128), 1)
     ).astype(jnp.bfloat16)
 
 
     def look(s):
+        to_smem[s].wait()
+
         def four(j, _):
             def some(i, _):
                 g = (me + 4 * j + i) % groups
                 for n in range(128):
-                    rows[pl.ds(i * 128 + n, 1), :] = major[pl.ds(spots_s[g, s, n], 1), :]
+                    rows[pl.ds(i * 128 + n, 1), :] = major[pl.ds(spots_s[s, g, n], 1), :]
                 return 0
 
             lax.fori_loop(0, 4, some, 0)
@@ -338,7 +405,7 @@
 
     length = lens_ref[me]
 
-    def block(s):
+    def prepare(s):
         for way in range(2):
             side(s, 2 + way).wait_recv()
         squares[...] = jnp.zeros_like(squares)
@@ -359,18 +426,21 @@
         def _():
             own_x[...] = xb[...]
 
+        here = slice(s * quarter, (s + 1) * quarter)
+
         def norm(c, _):
             cols = pl.ds(pl.multiple_of(c * 128, 128), 128)
             wide = xb[:, cols].astype(jnp.float32) * squares[...] * gain_ref[:, cols]
-            normed[:, cols] = wide.astype(jnp.bfloat16)
+            normed[here, cols] = wide.astype(jnp.bfloat16)
             return 0
 
         lax.fori_loop(0, width // 128, norm, 0, unroll=4)
-        here = slice(s * quarter, (s + 1) * quarter)
-
-        def project(b, first):
+    def project(lo, hi):
+        here = slice(lo * quarter, hi * quarter)
+
+        def product(b, first):
             return jnp.dot(
-                normed[...],
+                normed[here, :],
                 w[b, :, :, :, :, first : first + 256].reshape(width, 256),
                 preferred_element_type=jnp.float32,
             )
@@ -380,10 +450,10 @@
 
         def heads(b, _):
             for n in range(2):
-                both = project(b, n * 256)
+                both = product(b, n * 256)
                 for h in range(2):
-                    q[pl.ds(b * 4 + n * 2 + h, 1)] = rotated(both[:, h * HD : (h + 1) * HD])[None]
-            both = project(b, 512)
+                    q[pl.ds(b * 4 + n * 2 + h, 1), here] = rotated(both[:, h * HD : (h + 1) * HD])[None]
+            both = product(b, 512)
             k[pl.ds(b, 1), here] = rotated(both[:, :HD])[None]
             v[pl.ds(b, 1), here] = both[:, HD:].astype(jnp.bfloat16)[None]
             return 0
@@ -392,58 +462,65 @@
         for b in range(2):
             cache_ref[0, 0, here, b * HD : (b + 1) * HD] = k[b, here]
             cache_ref[0, 1, here, b * HD : (b + 1) * HD] = v[b, here]
+
+    def attend(s):
+        here = slice(s * quarter, (s + 1) * quarter)
         keys = (s + 1) * quarter
         p = lax.broadcasted_iota(jnp.int32, (quarter, keys), 0) + s * quarter
         j = lax.broadcasted_iota(jnp.int32, (quarter, keys), 1)
-        allowed = (j <= p) & (j < length)
-
-        def head(h, _):
-            b = h // 4
+        allowed = ((j <= p) & (j < length))[None]
+        for b in range(2):
             scores = lax.dot_general(
-                q[h], k[b, :keys], (((1,), (1,)), ((), ())), preferred_element_type=jnp.float32
-            )
+                q[b * 4 : b * 4 + 4, here].reshape(4 * quarter, HD),
+                k[b, :keys],
+                (((1,), (1,)), ((), ())),
+                preferred_element_type=jnp.float32,
+            ).reshape(4, quarter, keys)
             scores = jnp.where(allowed, scores * np.float32(1 / np.sqrt(HD)), -1e30)
-            expd = jnp.exp(scores - jnp.max(scores, axis=1, keepdims=True))
-            weights = (expd / jnp.sum(expd, axis=1, keepdims=True)).astype(jnp.bfloat16)
-            got = jnp.dot(weights, v[b, :keys], preferred_element_type=jnp.float32)
-            attended[here, pl.ds(pl.multiple_of(h * HD, HD), HD)] = got.astype(jnp.bfloat16)
-            return 0
-
-        lax.fori_loop(0, 8, head, 0, unroll=2)
-
+            expd = jnp.exp(scores - jnp.max(scores, axis=2, keepdims=True))
+            weights = (expd / jnp.sum(expd, axis=2, keepdims=True)).astype(jnp.bfloat16)
+            got = jnp.dot(weights.reshape(4 * quarter, keys), v[b, :keys], preferred_element_type=jnp.float32)
+            got = got.astype(jnp.bfloat16)
+            for h in range(4):
+                attended[here, (b * 4 + h) * HD : (b * 4 + h + 1) * HD] = got[h * quarter : (h + 1) * quarter]
+
+    plane_w.step(10)
+    plane_w.step(11)
     look(0)
-    plane_w.step(2)
+    plane_w.step(12)
     look(1)
     gather(0)
+    plane_w.step(13)
+    plane_w.step(14)
     look(2)
     gather(1)
     relay(0)
-    plane_w.step(3)
+    plane_w.step(15)
+    plane_w.step(16)
     look(3)
     gather(2)
+    plane_w.step(4)
     relay(1)
-    plane_w.step(4)
+    prepare(0)
     gather(3)
-    plane_o.step(0)
     plane_w.step(5)
+    relay(2)
+    plane_o.row_step(0)
     plane_w.step(6)
-    relay(2)
-    block(0)
+    prepare(1)
+    plane_o.row_step(1)
+    project(0, 2)
     relay(3)
-    plane_o.step(1)
-    block(1)
-    plane_o.step(2)
-    block(2)
-    plane_o.step(3)
-    plane_o.step(4)
-    block(3)
-    plane_o.step(5)
-    others.wait_send()
-    for s in range(4):
-        looked(s).wait_send()
-        for slot in range(4):
-            side(s, slot).wait_send()
-    plane_o.step(6)
+    prepare(2)
+    plane_o.row_step(2)
+    attend(0)
+    attend(1)
+    project(2, 3)
+    attend(2)
+    prepare(3)
+    plane_o.row_step(3)
+    project(3, 4)
+    attend(3)
 
 
     def far_copy(c, way):
@@ -466,12 +543,16 @@
             passed[pl.ds(c, 1), way] = total.astype(jnp.bfloat16)[None]
             sum_copy(c, way).start()
 
+    def row_of(c):
+        g = c // 2
+        return (z + g + g // 2 * (1 - 2 * (g % 2))) % 4
+
     def finish(c, _):
         for way in range(2):
             near_copy(c, way).wait_recv()
             sum_copy(c, way).wait_recv()
         for half in range(2):
-            cols = pl.ds(pl.multiple_of(c * 512 + half * 256, 256), 256)
+            cols = pl.ds(pl.multiple_of(row_of(c) * 1024 + c % 2 * 512 + half * 256, 256), 256)
             total = wide(stage[pl.ds(c, 1), pl.ds(y, 1), half])
             for way in range(2):
                 total = total + wide(final[pl.ds(c, 1), way, half])
@@ -482,8 +563,8 @@
 
     def output(c, _):
         for half in range(2):
-            part = jnp.dot(attended[:, :512], wo[0, c // 2, c % 2, half], preferred_element_type=jnp.float32)
-            part = part + jnp.dot(attended[:, 512:], wo[1, c // 2, c % 2, half], preferred_element_type=jnp.float32)
+            part = jnp.dot(attended[:, :512], wo[0, row_of(c), c % 2, half], preferred_element_type=jnp.float32)
+            part = part + jnp.dot(attended[:, 512:], wo[1, row_of(c), c % 2, half], preferred_element_type=jnp.float32)
             part = part.astype(jnp.bfloat16)
             for member in range(4):
                 stage[pl.ds(c, 1), member, half] = part[member * quarter : (member + 1) * quarter][None]
@@ -496,11 +577,32 @@
         def _():
             pass_on(c - 1)
 
+        @pl.when(c > 1)
+        def _():
+            finish(c - 2, 0)
+
         return 0
 
-    lax.fori_loop(0, chunks, output, 0)
+    plane_o.row_ready(0)
+    lax.fori_loop(0, 1, output, 0)
+    plane_o.row_step(4)
+    lax.fori_loop(1, 2, output, 0)
+    plane_o.row_ready(1)
+    lax.fori_loop(2, 4, output, 0)
+    plane_o.row_step(5)
+    plane_o.row_ready(3)
+    lax.fori_loop(4, 6, output, 0)
+    plane_o.row_ready(2)
+    lax.fori_loop(6, chunks, output, 0)
     pass_on(chunks - 1)
-    lax.fori_loop(0, chunks, finish, 0)
+    lax.fori_loop(chunks - 2, chunks, finish, 0)
+    others.wait_send()
+    for s in range(4):
+        looked(s).wait_send()
+        for slot in range(4):
+            side(s, slot).wait_send()
+    plane_w.drain()
+    plane_o.drain()
 
     def drain(c, _):
         for way in range(2):
@@ -540,17 +642,17 @@
             pltpu.VMEM((STRIP, 128), f32),
             pltpu.VMEM((512, 128), f32),
             pltpu.VMEM((groups, 4, 128), jnp.int32),
-            pltpu.VMEM((groups, 4, 128), jnp.int32),
-            pltpu.SMEM((groups, 4, 128), jnp.int32),
+            pltpu.VMEM((4, groups, 128), jnp.int32),
+            pltpu.SMEM((4, groups, 128), jnp.int32),
             pltpu.VMEM((4, groups, feats, 128), bf),
             pltpu.VMEM((4, groups, 4, feats, 128), bf),
             pltpu.VMEM((2, 4, 2, 2, depth, across), bf),
             pltpu.VMEM((2, 4, 2, 2, *w_out.shape), bf),
             pltpu.VMEM((quarter, width), bf),
             pltpu.VMEM((quarter, width), bf),
-            pltpu.VMEM((quarter, width), bf),
+            pltpu.VMEM((prompt, width), bf),
             pltpu.VMEM((quarter, 128), f32),
-            pltpu.VMEM((8, quarter, HD), bf),
+            pltpu.VMEM((8, prompt, HD), bf),
             pltpu.VMEM((2, prompt, HD), bf),
             pltpu.VMEM((2, prompt, HD), bf),
             pltpu.VMEM((prompt, 1024), bf),
@@ -559,7 +661,7 @@
             pltpu.VMEM((chunks, 2, quarter, 256), bf),
             pltpu.VMEM((chunks, 2, 2, quarter, 256), bf),
             dma((2, 4)),
-            dma,
+            dma((4,)),
             dma((4,)),
             dma((4,)),
             dma((4,)),

time: 141 us -> 125 us (0.89)
  Pallas kernels: 136 us -> 120 us
    pallas_call x1, Pallas kernels: 136 us -> 120 us  [shards(): pl.pallas_call(kernel, out_shape=(jax.ShapeDtypeStruct((quarter, width),...]
where the time goes in v6:
time: 125 us
  Pallas kernels  120 us (96%)
  local copies, waits for them, and re-layouts  4.16 us (3%)
    pallas_call x1, Pallas kernels, shards(): pl.pallas_call(kernel, out_shape=(jax.ShapeDtypeStruct((quarter, width),...  120 us
    unnamed x2, local copies, waits for them, and re-layouts  4.16 us

profile of v6, /device:TPU:0, one launch (start us, length us, event | category | flops | bytes accessed | tf_op | source)
XLA Modules:
  0.0 124.6 jit_solution(609189504465997673)
XLA Ops:
  0.6 119.8 %shard_map.113 = (bf16[128,4096]{1,0:T(8,128)(2,1)}, bf16[1,2,512,256]{3,2,1,0:T(8,128)(2,1)}) custom-call(s32[32]{0:T(128)} %lens_ref.1, s32[1,128]{1,0:T(1,128)} %bitcast.3, f32[1,4096]{1,0:T(1,128)} %bitcast.2, f32[512,128]{1,0:T(8,128)} %constant.4.clone.cos_ref, f32[512,128]{1,0:T(8,128)} %constant.5.clone.sin_ref, bf16[32,128256]{1,0:T(8,128)(2,1)} %table_ref.1, ...), custom_call_target="tpu_custom_call" | custom-call | tf_op jit(solution)/shard_map/pallas_call | solution.py:632
  120.4 2.3 %copy.14 = bf16[128,4096]{1,0:T(8,128)(2,1)} copy(bf16[128,4096]{1,0:T(8,128)(2,1)} %get-tuple-element.4) | data formatting | bytes 2097152
  122.7 1.9 %copy.15 = bf16[1,2,512,256]{3,2,1,0:T(8,128)(2,1)} copy(bf16[1,2,512,256]{3,2,1,0:T(8,128)(2,1)} %get-tuple-element.5) | data formatting | bytes 1048576

commit v7 on v6

--- a/solution.py
+++ b/solution.py
@@ -132,9 +132,9 @@
             self.start_full(2, 4)
         elif n == 2:
             self.take_relay(0)
-            self.start_full(3)
             self.take_full(1)
             self.start_cores(1, 0)
+            self.start_full(3)
         elif n == 3:
             for way in ways:
                 self.relay(0, 1, way).wait_recv()
@@ -169,50 +169,37 @@
 
     def step(self, n):
         if n == 0:
-            self.start_full(1)
-        elif n == -1:
             self.start_full(0)
         elif n == 1:
+            self.start_full(1)
+        elif n == 2:
             self.take_full(0)
-            self.start_full(2, 4)
-        elif n == 10:
-            self.take_full(0)
-        elif n == 11:
+        elif n == 3:
             self.start_full(2)
-        elif n == 12:
+        elif n == 4:
             self.start_full(4)
-        elif n == 13:
+        elif n == 5:
             self.take_relay(0)
             self.start_full(3)
-        elif n == 14:
+        elif n == 6:
             self.take_full(1)
-        elif n == 15:
+        elif n == 7:
+            self.start_cores(0, 0)
+            self.start_cores(1, 0)
+            self.take_full(2)
+        elif n == 8:
+            self.take_full(4)
+        elif n == 9:
+            self.take_full(3)
             for cls in range(2):
-                self.cores(cls, 0).start()
-            self.take_full(2)
-        elif n == 16:
-            self.take_full(4)
-        elif n == 2:
-            self.take_relay(0)
-            self.start_full(3)
-            self.take_full(1)
-        elif n == 3:
-            for cls in range(2):
-                self.cores(cls, 0).start()
-            self.take_full(2, 4)
-        elif n == 4:
-            self.take_full(3)
-            for o in (1, 3):
-                for cls in range(2):
-                    self.cores(cls, o).start()
-        elif n == 5:
+                self.start_cores(cls, 1, 3)
+        elif n == 10:
             self.take_relay(1, 2, 3, 4)
             for cls in range(2):
-                self.cores(cls, 2).start()
+                self.start_cores(cls, 2)
         else:
-            for cls in range(2):
-                for o in range(4):
-                    self.cores(cls, o).wait_recv()
+            for o in range(4):
+                self.row_ready(o)
 
     @staticmethod
     def sems():
@@ -224,9 +211,9 @@
     return (g // 8, g // 4 % 2, g // 2 % 2, g % 2, y)
 
 
-def kernel(lens_ref, ids_ref, gain_ref, cos_ref, sin_ref, table_ref, wq_ref, wk_ref, wv_ref, wo_ref, hidden_ref, cache_ref,
-           raw, major, rows, ids, spots, spots_s, staged, xt, w, wo, own_x, xb, normed, squares, q, k, v, attended,
-           stage, mid, passed, final, table_sems, spot_sem, own_sems, id_send, id_recv, look_send, look_recv,
+def kernel(lens_ref, ids_ref, gain_ref, trig_ref, table_ref, wq_ref, wk_ref, wv_ref, wo_ref, hidden_ref, cache_ref,
+           raw, major, rows, ids, spots, spots_s, staged, xt, w, wo, hidden, cache, own_x, xb, normed, trig, squares, q, k, v, attended,
+           stage, mid, passed, final, table_sems, spot_sem, own_sems, out_sems, id_send, id_recv, look_send, look_recv,
            side_send, side_recv, far_send, far_recv, near_send, near_recv, sum_send, sum_recv, *plane_sems):
     feats, vocab = table_ref.shape
     z = lax.axis_index("z")
@@ -236,7 +223,7 @@
     y = lax.axis_index("y")
     me = ((z * 2 + xlo) * 2 + core) * 2 + xhi
     groups = ids.shape[0]
-    quarter, width = hidden_ref.shape
+    quarter, width = hidden.shape
     up = (y + 1) % 4
     down = (y + 3) % 4
     far = (y + 2) % 4
@@ -277,6 +264,8 @@
         pltpu.make_async_copy(ref, own_w.at[:, pl.ds(first, ref.shape[1])], own_sems.at[n])
         for n, (ref, first) in enumerate(((wq_ref, 0), (wk_ref, 512), (wv_ref, 640)))
     ] + [pltpu.make_async_copy(wo_ref, own_wo, own_sems.at[3])]
+    angles = pltpu.make_async_copy(trig_ref, trig, own_sems.at[4])
+    angles.start()
     for copy in mine:
         copy.start()
     plane_w = Plane(w, own_w, plane_sems[:4])
@@ -304,7 +293,7 @@
 
         return 0
 
-    lax.fori_loop(0, 2, turn, 0)
+    lax.fori_loop(0, 1, turn, 0)
     pl.semaphore_wait(barrier, 3 + groups - 1)
     ids[pl.ds(me, 1), pl.ds(y, 1), :] = ids_ref[...][None]
     line = [
@@ -314,8 +303,8 @@
         copy.start()
     for copy in mine:
         copy.wait()
-    plane_w.step(-1)
-    lax.fori_loop(2, 5, turn, 0)
+    plane_w.step(0)
+    lax.fori_loop(1, 4, turn, 0)
     for copy in line:
         copy.wait()
 
@@ -324,8 +313,11 @@
         return 0
 
     lax.fori_loop(1, groups, spread, 0)
-    plane_w.step(0)
-    lax.fori_loop(5, LOADS, turn, 0)
+    plane_w.step(1)
+    lax.fori_loop(4, 9, turn, 0)
+    plane_w.step(2)
+    plane_w.step(3)
+    lax.fori_loop(9, LOADS, turn, 0)
     most = pl.ds(0, groups - 1)
     others = send(ids.at[most], ids.at[most], id_send.at[3], id_recv.at[3], at(up))
     others.wait_recv()
@@ -446,7 +438,7 @@
             )
 
         def rotated(part):
-            return (part * cos_ref[here, :] + pltpu.roll(part, HD // 2, 1) * sin_ref[here, :]).astype(jnp.bfloat16)
+            return (part * trig[0, here, :] + pltpu.roll(part, HD // 2, 1) * trig[1, here, :]).astype(jnp.bfloat16)
 
         def heads(b, _):
             for n in range(2):
@@ -460,8 +452,8 @@
 
         lax.fori_loop(0, 2, heads, 0)
         for b in range(2):
-            cache_ref[0, 0, here, b * HD : (b + 1) * HD] = k[b, here]
-            cache_ref[0, 1, here, b * HD : (b + 1) * HD] = v[b, here]
+            cache[0, 0, here, b * HD : (b + 1) * HD] = k[b, here]
+            cache[0, 1, here, b * HD : (b + 1) * HD] = v[b, here]
 
     def attend(s):
         here = slice(s * quarter, (s + 1) * quarter)
@@ -484,37 +476,37 @@
             for h in range(4):
                 attended[here, (b * 4 + h) * HD : (b * 4 + h + 1) * HD] = got[h * quarter : (h + 1) * quarter]
 
-    plane_w.step(10)
-    plane_w.step(11)
     look(0)
-    plane_w.step(12)
+    plane_w.step(4)
     look(1)
     gather(0)
-    plane_w.step(13)
-    plane_w.step(14)
+    plane_w.step(5)
+    plane_w.step(6)
     look(2)
     gather(1)
     relay(0)
-    plane_w.step(15)
-    plane_w.step(16)
+    plane_w.step(7)
+    plane_w.step(8)
     look(3)
     gather(2)
-    plane_w.step(4)
+    plane_w.step(9)
     relay(1)
     prepare(0)
     gather(3)
-    plane_w.step(5)
+    plane_o.row_step(0)
+    plane_w.step(10)
     relay(2)
-    plane_o.row_step(0)
-    plane_w.step(6)
+    plane_w.step(11)
+    angles.wait()
+    project(0, 1)
+    plane_o.row_step(1)
+    attend(0)
     prepare(1)
-    plane_o.row_step(1)
-    project(0, 2)
+    project(1, 2)
+    attend(1)
     relay(3)
     prepare(2)
     plane_o.row_step(2)
-    attend(0)
-    attend(1)
     project(2, 3)
     attend(2)
     prepare(3)
@@ -546,6 +538,10 @@
     def row_of(c):
         g = c // 2
         return (z + g + g // 2 * (1 - 2 * (g % 2))) % 4
+
+    def leave(c):
+        cols = pl.ds(pl.multiple_of(row_of(c) * 1024 + c % 2 * 512, 512), 512)
+        return pltpu.make_async_copy(hidden.at[:, cols], hidden_ref.at[:, cols], out_sems.at[c])
 
     def finish(c, _):
         for way in range(2):
@@ -556,7 +552,8 @@
             total = wide(stage[pl.ds(c, 1), pl.ds(y, 1), half])
             for way in range(2):
                 total = total + wide(final[pl.ds(c, 1), way, half])
-            hidden_ref[:, cols] = (own_x[:, cols].astype(jnp.float32) + total).astype(jnp.bfloat16)
+            hidden[:, cols] = (own_x[:, cols].astype(jnp.float32) + total).astype(jnp.bfloat16)
+        leave(c).start()
         return 0
 
     chunks = stage.shape[0]
@@ -584,18 +581,16 @@
         return 0
 
     plane_o.row_ready(0)
+    cache_out = pltpu.make_async_copy(cache, cache_ref, own_sems.at[5])
     lax.fori_loop(0, 1, output, 0)
     plane_o.row_step(4)
+    cache_out.start()
     lax.fori_loop(1, 2, output, 0)
     plane_o.row_ready(1)
     lax.fori_loop(2, 4, output, 0)
     plane_o.row_step(5)
     plane_o.row_ready(3)
     lax.fori_loop(4, 6, output, 0)
-    plane_o.row_ready(2)
-    lax.fori_loop(6, chunks, output, 0)
-    pass_on(chunks - 1)
-    lax.fori_loop(chunks - 2, chunks, finish, 0)
     others.wait_send()
     for s in range(4):
         looked(s).wait_send()
@@ -603,15 +598,20 @@
             side(s, slot).wait_send()
     plane_w.drain()
     plane_o.drain()
-
+    plane_o.row_ready(2)
+    lax.fori_loop(6, chunks, output, 0)
+    pass_on(chunks - 1)
+    lax.fori_loop(chunks - 2, chunks, finish, 0)
     def drain(c, _):
         for way in range(2):
             far_copy(c, way).wait_send()
             near_copy(c, way).wait_send()
             sum_copy(c, way).wait_send()
+        leave(c).wait()
         return 0
 
     lax.fori_loop(0, chunks, drain, 0)
+    cache_out.wait()
 
 
 def shards(prompt_ids, prompt_lengths, embed_table, norm_gain, w_query, w_key, w_value, w_out):
@@ -635,8 +635,8 @@
             jax.ShapeDtypeStruct((quarter, width), bf),
             jax.ShapeDtypeStruct((1, 2, prompt, 2 * HD), bf),
         ),
-        in_specs=[pl.BlockSpec(memory_space=pltpu.SMEM)] + [vmem] * 4 + [anyw] * 5,
-        out_specs=(vmem, vmem),
+        in_specs=[pl.BlockSpec(memory_space=pltpu.SMEM)] + [vmem] * 2 + [anyw] * 6,
+        out_specs=(anyw, anyw),
         scratch_shapes=[
             pltpu.VMEM((2, 4, feats, TILES * 128), bf),
             pltpu.VMEM((STRIP, 128), f32),
@@ -649,8 +649,11 @@
             pltpu.VMEM((2, 4, 2, 2, depth, across), bf),
             pltpu.VMEM((2, 4, 2, 2, *w_out.shape), bf),
             pltpu.VMEM((quarter, width), bf),
+            pltpu.VMEM((1, 2, prompt, 2 * HD), bf),
+            pltpu.VMEM((quarter, width), bf),
             pltpu.VMEM((quarter, width), bf),
             pltpu.VMEM((prompt, width), bf),
+            pltpu.VMEM((2, prompt, HD), f32),
             pltpu.VMEM((quarter, 128), f32),
             pltpu.VMEM((8, prompt, HD), bf),
             pltpu.VMEM((2, prompt, HD), bf),
@@ -662,7 +665,8 @@
             pltpu.VMEM((chunks, 2, 2, quarter, 256), bf),
             dma((2, 4)),
             dma((4,)),
-            dma((4,)),
+            dma((6,)),
+            dma((chunks,)),
             dma((4,)),
             dma((4,)),
             dma((4,)),
@@ -678,8 +682,7 @@
         prompt_lengths,
         prompt_ids.reshape(1, quarter),
         norm_gain.reshape(1, width),
-        cosine,
-        sine,
+        np.stack([cosine, sine]),
         embed_table,
         w_query,
         w_key,

time: 125 us -> 123 us (0.984)
  Pallas kernels: 120 us -> 117 us
    pallas_call x1, Pallas kernels: 120 us -> 117 us  [shards(): pl.pallas_call(kernel, out_shape=(jax.ShapeDtypeStruct((quarter, width),...]
where the time goes in v7:
time: 123 us; the launch traced here: 122 us
  Pallas kernels  117 us (95%)
  local copies, waits for them, and re-layouts  4.16 us (3%)
    pallas_call x1, Pallas kernels, shards(): pl.pallas_call(kernel, out_shape=(jax.ShapeDtypeStruct((quarter, width),...  117 us
    unnamed x2, local copies, waits for them, and re-layouts  4.16 us

profile of v7, /device:TPU:0, one launch (start us, length us, event | category | flops | bytes accessed | tf_op | source)
XLA Modules:
  0.0 122.1 jit_solution(7117196604853225119)
XLA Ops:
  0.6 117.3 %shard_map.104 = (bf16[128,4096]{1,0:T(8,128)(2,1)}, bf16[1,2,512,256]{3,2,1,0:T(8,128)(2,1)}) custom-call(s32[32]{0:T(128)} %lens_ref.1, s32[1,128]{1,0:T(1,128)} %bitcast.3, f32[1,4096]{1,0:T(1,128)} %bitcast.2, f32[2,512,128]{2,1,0:T(8,128)} %constant.2.clone.trig_ref, bf16[32,128256]{1,0:T(8,128)(2,1)} %table_ref.1, bf16[256,512]{1,0:T(8,128)(2,1)} %wq_ref.1, ...), custom_call_target="tpu_custom_call" | custom-call | tf_op jit(solution)/shard_map/pallas_call | solution.py:632
  117.9 2.3 %copy.13 = bf16[128,4096]{1,0:T(8,128)(2,1)} copy(bf16[128,4096]{1,0:T(8,128)(2,1)} %get-tuple-element.4) | data formatting | bytes 2097152
  120.2 1.9 %copy.14 = bf16[1,2,512,256]{3,2,1,0:T(8,128)(2,1)} copy(bf16[1,2,512,256]{3,2,1,0:T(8,128)(2,1)} %get-tuple-element.5) | data formatting | bytes 1048576

commit v8 on v7

--- a/solution.py
+++ b/solution.py
@@ -614,6 +614,42 @@
     cache_out.wait()
 
 
+def settle_kernel(first_ref, second_ref, first_out, second_out, first, second, sems):
+    pieces = []
+    for n in range(4):
+        part = pl.ds(n * (first.shape[0] // 4), first.shape[0] // 4)
+        pieces.append((first_ref.at[part], first.at[part], first_out.at[part]))
+    for n in range(2):
+        pieces.append((second_ref.at[0, n], second.at[0, n], second_out.at[0, n]))
+    ways = [
+        (pltpu.make_async_copy(a, b, sems.at[0, n]), pltpu.make_async_copy(b, c, sems.at[1, n]))
+        for n, (a, b, c) in enumerate(pieces)
+    ]
+    for into, _ in ways:
+        into.start()
+    for into, out in ways:
+        into.wait()
+        out.start()
+    for _, out in ways:
+        out.wait()
+
+
+def settle(first, second):
+    anyw = pl.BlockSpec(memory_space=pl.ANY)
+    return pl.pallas_call(
+        settle_kernel,
+        out_shape=(jax.ShapeDtypeStruct(first.shape, first.dtype), jax.ShapeDtypeStruct(second.shape, second.dtype)),
+        in_specs=[anyw, anyw],
+        out_specs=(anyw, anyw),
+        scratch_shapes=[
+            pltpu.VMEM(first.shape, first.dtype),
+            pltpu.VMEM(second.shape, second.dtype),
+            pltpu.SemaphoreType.DMA((2, 6)),
+        ],
+        compiler_params=pltpu.CompilerParams(vmem_limit_bytes=67043328),
+    )(first, second)
+
+
 def shards(prompt_ids, prompt_lengths, embed_table, norm_gain, w_query, w_key, w_value, w_out):
     quarter = prompt_ids.shape[0]
     prompt = quarter * 4
@@ -629,7 +665,7 @@
     vmem = pl.BlockSpec(memory_space=pltpu.VMEM)
     anyw = pl.BlockSpec(memory_space=pl.ANY)
     dma = pltpu.SemaphoreType.DMA
-    return pl.pallas_call(
+    hidden, cache = pl.pallas_call(
         kernel,
         out_shape=(
             jax.ShapeDtypeStruct((quarter, width), bf),
@@ -689,6 +725,7 @@
         w_value,
         w_out,
     )
+    return settle(hidden, cache)
 
 
 def solution(mesh):

time: 123 us -> 121 us (0.984)
  local copies, waits for them, and re-layouts: 4.16 us -> 0 us
  Pallas kernels: 117 us -> 119 us
    unnamed x2 -> x0, local copies, waits for them, and re-layouts: 4.16 us -> none
    pallas_call x0 -> x1, Pallas kernels: none -> 2.19 us  [settle(): pl.pallas_call(settle_kernel, out_shape=(jax.ShapeDtypeStruct(first.shape...]
where the time goes in v8:
time: 121 us; the launch traced here: 120 us
  Pallas kernels  119 us (98%)
    pallas_call x1, Pallas kernels, shards(): pl.pallas_call(kernel, out_shape=(jax.ShapeDtypeStruct((quarter, width),...  117 us

profile of v8, /device:TPU:0, one launch (start us, length us, event | category | flops | bytes accessed | tf_op | source)
XLA Modules:
  0.0 120.3 jit_solution(18137059189041296335)
XLA Ops:
  0.6 117.3 %shard_map.104 = (bf16[128,4096]{1,0:T(8,128)(2,1)}, bf16[1,2,512,256]{3,2,1,0:T(8,128)(2,1)}) custom-call(s32[32]{0:T(128)} %lens_ref.1, s32[1,128]{1,0:T(1,128)} %bitcast.3, f32[1,4096]{1,0:T(1,128)} %bitcast.2, f32[2,512,128]{2,1,0:T(8,128)} %constant.2.clone.trig_ref, bf16[32,128256]{1,0:T(8,128)(2,1)} %table_ref.1, bf16[256,512]{1,0:T(8,128)(2,1)} %wq_ref.1, ...), custom_call_target="tpu_custom_call" | custom-call | tf_op jit(solution)/shard_map/pallas_call | solution.py:668
  117.9 2.2 %shard_map.105 = (bf16[128,4096]{1,0:T(8,128)(2,1)}, bf16[1,2,512,256]{3,2,1,0:T(8,128)(2,1)}) custom-call(bf16[128,4096]{1,0:T(8,128)(2,1)} %get-tuple-element.4.first_ref, bf16[1,2,512,256]{3,2,1,0:T(8,128)(2,1)} %get-tuple-element.5.second_ref), custom_call_target="tpu_custom_call" | custom-call | tf_op jit(solution)/shard_map/pallas_call | solution.py:639

commit v9 on v8

--- a/solution.py
+++ b/solution.py
@@ -496,15 +496,14 @@
     plane_o.row_step(0)
     plane_w.step(10)
     relay(2)
+    prepare(1)
     plane_w.step(11)
+    plane_o.row_step(1)
     angles.wait()
-    project(0, 1)
-    plane_o.row_step(1)
+    project(0, 2)
     attend(0)
-    prepare(1)
-    project(1, 2)
+    relay(3)
     attend(1)
-    relay(3)
     prepare(2)
     plane_o.row_step(2)
     project(2, 3)

time: 121 us -> 120 us (level)
  no operation moved by 1% of the time
where the time goes in v9:
time: 120 us
  Pallas kernels  119 us (99%)
    pallas_call x1, Pallas kernels, shards(): pl.pallas_call(kernel, out_shape=(jax.ShapeDtypeStruct((quarter, width),...  117 us

profile of v9, /device:TPU:0, one launch (start us, length us, event | category | flops | bytes accessed | tf_op | source)
XLA Modules:
  0.0 119.6 jit_solution(14095294403384655471)
XLA Ops:
  0.6 116.6 %shard_map.104 = (bf16[128,4096]{1,0:T(8,128)(2,1)}, bf16[1,2,512,256]{3,2,1,0:T(8,128)(2,1)}) custom-call(s32[32]{0:T(128)} %lens_ref.1, s32[1,128]{1,0:T(1,128)} %bitcast.3, f32[1,4096]{1,0:T(1,128)} %bitcast.2, f32[2,512,128]{2,1,0:T(8,128)} %constant.2.clone.trig_ref, bf16[32,128256]{1,0:T(8,128)(2,1)} %table_ref.1, bf16[256,512]{1,0:T(8,128)(2,1)} %wq_ref.1, ...), custom_call_target="tpu_custom_call" | custom-call | tf_op jit(solution)/shard_map/pallas_call | solution.py:667
  117.3 2.2 %shard_map.105 = (bf16[128,4096]{1,0:T(8,128)(2,1)}, bf16[1,2,512,256]{3,2,1,0:T(8,128)(2,1)}) custom-call(bf16[128,4096]{1,0:T(8,128)(2,1)} %get-tuple-element.4.first_ref, bf16[1,2,512,256]{3,2,1,0:T(8,128)(2,1)} %get-tuple-element.5.second_ref), custom_call_target="tpu_custom_call" | custom-call | tf_op jit(solution)/shard_map/pallas_call | solution.py:638

commit v10 on v9

--- a/solution.py
+++ b/solution.py
@@ -497,8 +497,8 @@
     plane_w.step(10)
     relay(2)
     prepare(1)
+    plane_o.row_step(1)
     plane_w.step(11)
-    plane_o.row_step(1)
     angles.wait()
     project(0, 2)
     attend(0)

time: 120 us -> 120 us (level)
  no operation moved by 1% of the time
where the time goes in v10:
time: 120 us
  Pallas kernels  119 us (99%)
    pallas_call x1, Pallas kernels, shards(): pl.pallas_call(kernel, out_shape=(jax.ShapeDtypeStruct((quarter, width),...  117 us

profile of v10, /device:TPU:0, one launch (start us, length us, event | category | flops | bytes accessed | tf_op | source)
XLA Modules:
  0.0 119.6 jit_solution(3356047409745863000)
XLA Ops:
  0.6 116.6 %shard_map.104 = (bf16[128,4096]{1,0:T(8,128)(2,1)}, bf16[1,2,512,256]{3,2,1,0:T(8,128)(2,1)}) custom-call(s32[32]{0:T(128)} %lens_ref.1, s32[1,128]{1,0:T(1,128)} %bitcast.3, f32[1,4096]{1,0:T(1,128)} %bitcast.2, f32[2,512,128]{2,1,0:T(8,128)} %constant.2.clone.trig_ref, bf16[32,128256]{1,0:T(8,128)(2,1)} %table_ref.1, bf16[256,512]{1,0:T(8,128)(2,1)} %wq_ref.1, ...), custom_call_target="tpu_custom_call" | custom-call | tf_op jit(solution)/shard_map/pallas_call | solution.py:667
  117.3 2.2 %shard_map.105 = (bf16[128,4096]{1,0:T(8,128)(2,1)}, bf16[1,2,512,256]{3,2,1,0:T(8,128)(2,1)}) custom-call(bf16[128,4096]{1,0:T(8,128)(2,1)} %get-tuple-element.4.first_ref, bf16[1,2,512,256]{3,2,1,0:T(8,128)(2,1)} %get-tuple-element.5.second_ref), custom_call_target="tpu_custom_call" | custom-call | tf_op jit(solution)/shard_map/pallas_call | solution.py:638
